TPU v7x, 32 devices: a whole 2x2x4 slice. The times are simulated.
32 devices in a mesh: tx: 8 (over y, x, core), ty: 4 (over z).
Axes of the slice: x: 2, y: 2, z: 4, core: 2. Of those that a mesh axis runs over, the one named last changes fastest.
Arguments:
- mag: float32 [3, 2048, 2048], P(None, 'tx', 'ty'), may hold values from -1 to 1, as said below
- occupancy: int32 [2048, 2048], P('tx', 'ty'), may hold values from 0 to 1
- kernel_spectrum: float32 [4, 4096, 4096], P(None, ('tx', 'ty')), may hold values from -0.5 to 1, as said below
Outputs:
- mag_next: float32 [3, 2048, 2048], P(None, 'tx', 'ty')
- mean_rate: float32 [3, 2048, 2048], P(None, 'tx', 'ty')
Inputs may be any that keep to these rules, and one draw needn't show every extreme that they name: `mag`: each cell's three components have unit length. `kernel_spectrum`: each component is unchanged under (y frequency, x frequency) -> ((4096 - y frequency) mod 2 * 2048, (4096 - x frequency) mod 2 * 2048).
All inputs are finite; a program needn't handle non-finite values.
Results may differ from a plain program's by a relative error of at most 0.00005.
Values sent between devices are 32-bit elements; how exact they have to be, the bound alone decides.
No kernel may reach another device: no remote copies, remote signals or barrier semaphores. Data moves between devices by JAX's collectives and lax.ppermute only.
A program may use at most 192 MiB of HBM per device.

v0:
```python
import math

import jax
import jax.numpy as jnp
from jax import lax
from jax.sharding import PartitionSpec as P

DAMPING = 0.3
STIFFNESS = 0.25
TIME_STEP = 0.25


def padded_2(array, sides, width):
    for axis, dim in sides:
        size, length = (lax.axis_size(axis), array.shape[dim])
        up = [(i, (i + 1) % size) for i in range(size - 1)]
        down = [(j, i) for i, j in up]
        last = lax.slice_in_dim(array, length - width, length, axis=dim)
        initial = lax.slice_in_dim(array, 0, width, axis=dim)
        before = lax.ppermute(last, axis, up)
        after = lax.ppermute(initial, axis, down)
        array = jnp.concatenate([before, array, after], axis=dim)
    return array


def contract(form, left, right):
    return jnp.einsum(form, left, right, precision=lax.Precision.HIGHEST)


def trig(first_count, second_count, length):
    first_index = jnp.arange(first_count, dtype=jnp.int32)
    second_index = jnp.arange(second_count, dtype=jnp.int32)
    product = first_index[:, None] * second_index[None, :] % length
    angle = product.astype(jnp.float32) * (2.0 * math.pi / length)
    return (jnp.cos(angle), jnp.sin(angle))


def factors(length):
    bits = length.bit_length() - 1
    outer_len = 1 << bits // 2
    return (length // outer_len, outer_len)


def turn(values):
    paired = values.reshape(values.shape[:-1] + (values.shape[-1] // 2, 2))
    return jnp.stack([-paired[..., 1], paired[..., 0]], axis=-1).reshape(values.shape)


def y_forward(rows):
    comps, row_count, width = rows.shape
    length = 2 * width
    first_len, second_len = factors(length)
    shaped = rows.reshape(comps, row_count, first_len // 2, second_len)
    cos_one, sin_one = trig(first_len // 2, first_len, first_len)
    real_part = contract("mrab,ac->rbcm", shaped, cos_one)
    imag_part = -contract("mrab,ac->rbcm", shaped, sin_one)
    section = jnp.stack([real_part, imag_part], axis=-1).reshape(
        row_count, second_len, first_len, 2 * comps
    )
    twist_cos, twist_sin = trig(second_len, first_len, length)
    section = section * twist_cos[None, :, :, None] - turn(section) * twist_sin[None, :, :, None]
    cos_two, sin_two = trig(second_len, second_len, second_len)
    result = contract("rbcz,bd->rdcz", section, cos_two) - contract(
        "rbcz,bd->rdcz", turn(section), sin_two
    )
    return result.reshape(row_count, length * 2 * comps)


def x_forward(columns):
    half, width = columns.shape
    length = 2 * half
    first_len, second_len = factors(length)
    shaped = columns.reshape(first_len // 2, second_len, width)
    cos_one, sin_one = trig(first_len // 2, first_len, first_len)
    section = contract("abz,ac->cbz", shaped, cos_one) - contract(
        "abz,ac->cbz", turn(shaped), sin_one
    )
    twist_cos, twist_sin = trig(first_len, second_len, length)
    section = section * twist_cos[:, :, None] - turn(section) * twist_sin[:, :, None]
    cos_two, sin_two = trig(second_len, second_len, second_len)
    result = contract("cbz,bd->dcz", section, cos_two) - contract(
        "cbz,bd->dcz", turn(section), sin_two
    )
    return result.reshape(length, width)


def x_inverse(spectra):
    length, width = spectra.shape
    first_len, second_len = factors(length)
    shaped = spectra.reshape(second_len, first_len, width)
    cos_one, sin_one = trig(second_len, second_len, second_len)
    section = contract("dcz,db->bcz", shaped, cos_one) + contract(
        "dcz,db->bcz", turn(shaped), sin_one
    )
    twist_cos, twist_sin = trig(second_len, first_len, length)
    section = section * twist_cos[:, :, None] + turn(section) * twist_sin[:, :, None]
    cos_two, sin_two = trig(first_len, first_len // 2, first_len)
    result = contract("bcz,ca->abz", section, cos_two) + contract(
        "bcz,ca->abz", turn(section), sin_two
    )
    return result.reshape(length // 2, width) * (1.0 / length)


def y_inverse(spectra):
    row_count = spectra.shape[0]
    length = spectra.shape[1] // 6
    first_len, second_len = factors(length)
    shaped = spectra.reshape(row_count, second_len, first_len, 6)
    cos_one, sin_one = trig(second_len, second_len, second_len)
    section = contract("rdcz,db->rbcz", shaped, cos_one) + contract(
        "rdcz,db->rbcz", turn(shaped), sin_one
    )
    twist_cos, twist_sin = trig(second_len, first_len, length)
    section = section * twist_cos[None, :, :, None] + turn(section) * twist_sin[None, :, :, None]
    parts = section.reshape(row_count, second_len, first_len, 3, 2)
    cos_two, sin_two = trig(first_len, first_len // 2, first_len)
    result = contract("rbcm,ca->mrab", parts[..., 0], cos_two) - contract(
        "rbcm,ca->mrab", parts[..., 1], sin_two
    )
    return result.reshape(3, row_count, length // 2) * (1.0 / length)


def cross(left, right):
    return jnp.stack(
        [
            left[1] * right[2] - left[2] * right[1],
            left[2] * right[0] - left[0] * right[2],
            left[0] * right[1] - left[1] * right[0],
        ]
    )


def rim_sum(padded):
    return (
        padded[..., 2:, 1:-1]
        + padded[..., :-2, 1:-1]
        + padded[..., 1:-1, 2:]
        + padded[..., 1:-1, :-2]
    )


def send_out(spectra):
    return lax.all_to_all(spectra, ("tx", "ty"), split_axis=1, concat_axis=0, tiled=True)


def send_back(partial_value):
    return lax.all_to_all(partial_value, ("tx", "ty"), split_axis=0, concat_axis=1, tiled=True)


def apply_kernel(kernel, spectra):
    length, width = spectra.shape
    split = spectra.reshape(length, width // 6, 3, 2)
    gains = kernel[..., None]
    field_x = -(gains[0] * split[:, :, 0] + gains[3] * split[:, :, 1])
    field_y = -(gains[3] * split[:, :, 0] + gains[1] * split[:, :, 1])
    field_z = -(gains[2] * split[:, :, 2])
    return jnp.stack([field_x, field_y, field_z], axis=2).reshape(length, width)


def demag(field, kernel):
    rows = lax.all_to_all(field, "ty", split_axis=1, concat_axis=2, tiled=True)
    spectra = y_forward(rows)
    columns = send_out(spectra)
    product = apply_kernel(kernel, x_forward(columns))
    partial_value = x_inverse(product)
    returned = send_back(partial_value)
    spatial = y_inverse(returned)
    return lax.all_to_all(spatial, "ty", split_axis=2, concat_axis=1, tiled=True)


def body(mag, occupancy, kernel_spectrum):
    occ = occupancy.astype(jnp.float32)
    start = mag * occ[None]
    kernel = jnp.transpose(kernel_spectrum, (0, 2, 1))

    def rate(field):
        padded = padded_2(field, (("tx", 1), ("ty", 2)), 1)
        effective = demag(field, kernel) + STIFFNESS * rim_sum(padded)
        torque = cross(field, effective)
        return -(torque + DAMPING * cross(field, torque)) / (1.0 + DAMPING * DAMPING)

    def normal(vector):
        return vector / jnp.sqrt(jnp.sum(vector * vector, axis=0) + 1.0 - occ)[None]

    first = rate(start)
    middle = normal(start + TIME_STEP * first)
    second = rate(middle)
    second = second - jnp.sum(second * start, axis=0)[None] * start
    mean_rate = 0.5 * (first + second)
    mag_next = normal(start + TIME_STEP * mean_rate)
    return (mag_next, mean_rate)


def solution(mesh):
    return jax.shard_map(
        body,
        mesh=mesh,
        in_specs=(P(None, "tx", "ty"), P("tx", "ty"), P(None, ("tx", "ty"), None)),
        out_specs=(P(None, "tx", "ty"), P(None, "tx", "ty")),
        check_vma=False,
    )
```

profile of v0, /device:TPU:0, one launch (start us, length us, event | category | flops | bytes accessed | tf_op | source)
XLA Modules:
  0.0 3034.0 jit_solution(8483581114872307505)
XLA Ops:
  14.4 47.9 %all-to-all-done = f32[3,256,512]{2,0,1:T(4,128)S(1)} async-done(((f32[3,256,512]{2,0,1:T(4,128)}), f32[3,256,512]{2,0,1:T(4,128)S(1)}, u32[]{:S(2)}, u32[]{:S(2)}) %all-to-all-start) | async-done | bytes 1572896 | tf_op jit(solution)/shard_map/all_to_all | solution.py:161
  242.6 129.6 %all-to-all-done.1 = f32[64,32,768]{2,0,1:T(8,128)} async-done(((f32[64,32,768]{2,0,1:T(8,128)}), f32[64,32,768]{2,0,1:T(8,128)}, u32[]{:S(2)}, u32[]{:S(2)}) %all-to-all-start.1) | async-done | bytes 6291488 | tf_op jit(solution)/shard_map/all_to_all | solution.py:143
  451.3 23.7 copy.161
  540.3 23.7 copy.164
  593.6 54.4 %fusion.6 = f32[64,64,768]{2,0,1:T(8,128)} fusion(f32[64,64,768]{1,0,2:T(8,128)} %bitcast.292), kind=kOutput, calls=%fused_computation.16 | convolution fusion | flops 2415976448 | bytes 25165824 | tf_op jit(solution)/shard_map/cbz,bd->dcz/dot_general | solution.py:27
  648.0 27.1 fusion.48
  675.1 23.7 copy.166
  894.5 23.7 copy.169
  984.1 23.7 copy.172
  1047.6 49.3 %fusion.4 = f32[32,64,768]{2,0,1:T(8,128)} fusion(f32[64,64,768]{1,0,2:T(8,128)} %bitcast.305), kind=kOutput, calls=%fused_computation.14 | convolution fusion | flops 1207988224 | bytes 18874368 | tf_op jit(solution)/shard_map/bcz,ca->abz/dot_general | solution.py:27
  1116.4 144.3 %all_to_all.124 = f32[32,64,768]{2,1,0:T(8,128)} all-to-all(f32[32,64,768]{2,1,0:T(8,128)S(1)} %copy.174), channel_id=1, replica_groups=mesh['tx'=8,'ty'=4] {'tx','ty'}, dimensions={0} | all-to-all | bytes 12582912 | tf_op jit(solution)/shard_map/all_to_all | solution.py:147
  1476.2 25.2 all-to-all-done.3
  1526.3 51.0 %all_to_all.125 = f32[3,256,512]{2,0,1:T(4,128)S(1)} all-to-all(f32[3,256,512]{2,0,1:T(4,128)S(1)} %copy.184), channel_id=1, replica_groups=mesh['tx'=8,'ty'=4] {'ty'}, dimensions={1} | all-to-all | bytes 3145728 | tf_op jit(solution)/shard_map/all_to_all | solution.py:161
  1743.8 140.9 %all_to_all.126 = f32[64,32,768]{2,0,1:T(8,128)} all-to-all(f32[64,32,768]{2,0,1:T(8,128)} %copy.190), channel_id=1, replica_groups=mesh['tx'=8,'ty'=4] {'tx','ty'}, dimensions={1} | all-to-all | bytes 12582912 | tf_op jit(solution)/shard_map/all_to_all | solution.py:143
  1960.0 23.7 copy.194
  2049.2 23.7 copy.197
  2102.5 54.4 %fusion.2 = f32[64,64,768]{2,0,1:T(8,128)} fusion(f32[64,64,768]{1,0,2:T(8,128)} %bitcast.300), kind=kOutput, calls=%fused_computation.12 | convolution fusion | flops 2415976448 | bytes 25165824 | tf_op jit(solution)/shard_map/cbz,bd->dcz/dot_general | solution.py:27
  2156.8 27.1 fusion.51
  2184.0 23.7 copy.199
  2403.5 23.7 copy.202
  2492.7 23.7 copy.205
  2556.2 49.4 %fusion = f32[32,64,768]{2,0,1:T(8,128)} fusion(f32[64,64,768]{1,0,2:T(8,128)} %bitcast.306), kind=kOutput, calls=%fused_computation.10 | convolution fusion | flops 1207988224 | bytes 18874368 | tf_op jit(solution)/shard_map/bcz,ca->abz/dot_general | solution.py:27
  2625.0 141.9 %all_to_all.127 = f32[32,64,768]{2,1,0:T(8,128)} all-to-all(f32[32,64,768]{2,1,0:T(8,128)S(1)} %copy.207), channel_id=1, replica_groups=mesh['tx'=8,'ty'=4] {'tx','ty'}, dimensions={0} | all-to-all | bytes 12582912 | tf_op jit(solution)/shard_map/all_to_all | solution.py:147
  2982.5 25.1 all-to-all-done.7
  (294 shorter events, 1827.1 us)
Async XLA Ops:
  7.7 54.5 %all-to-all-start = ((f32[3,256,512]{2,0,1:T(4,128)}), f32[3,256,512]{2,0,1:T(4,128)S(1)}, u32[]{:S(2)}, u32[]{:S(2)}) async-start(f32[3,256,512]{2,0,1:T(4,128)} %copy.149), calls=%async_computation | async-start | bytes 4194304 | tf_op jit(solution)/shard_map/all_to_all | solution.py:161
  14.2 69.2 %copy-start.28 = (f32[64,64]{0,1:T(8,128)}, f32[64,64]{0,1:T(8,128)S(1)}, u32[]{:S(2)}) copy-start(f32[64,64]{0,1:T(8,128)S(1)} %get-tuple-element.74) | copy-start | bytes 49156
  14.2 69.1 %copy-start.34 = (f32[64,64]{0,1:T(8,128)}, f32[64,64]{0,1:T(8,128)S(1)}, u32[]{:S(2)}) copy-start(f32[64,64]{0,1:T(8,128)S(1)} %get-tuple-element.75) | copy-start | bytes 49156
  14.3 143.0 %copy-start.40 = (f32[64,64]{1,0:T(8,128)}, f32[64,64]{1,0:T(8,128)S(1)}, u32[]{:S(2)}) copy-start(f32[64,64]{1,0:T(8,128)S(1)} %copy.152) | copy-start | bytes 49156
  14.4 142.9 %copy-start.43 = (f32[64,64]{1,0:T(8,128)}, f32[64,64]{1,0:T(8,128)S(1)}, u32[]{:S(2)}) copy-start(f32[64,64]{1,0:T(8,128)S(1)} %copy.154) | copy-start | bytes 49156
  231.7 140.6 %all-to-all-start.1 = ((f32[64,32,768]{2,0,1:T(8,128)}), f32[64,32,768]{2,0,1:T(8,128)}, u32[]{:S(2)}, u32[]{:S(2)}) async-start(f32[64,32,768]{2,0,1:T(8,128)} %copy.157), calls=%async_computation.1 | async-start | bytes 12582912 | tf_op jit(solution)/shard_map/all_to_all | solution.py:143
  1027.5 69.5 %slice-start.3 = ((s8[12582912]{0:T(1024)(128)(4,1)}), s8[4194304]{0:T(1024)(128)(4,1)S(1)}, s32[]{:S(2)}) async-start(s8[12582912]{0:T(1024)(128)(4,1)} %bitcast.285), calls=%async_computation.11 | async-start | bytes 8388608
  1027.5 69.5 %slice-start.4 = ((s8[12582912]{0:T(1024)(128)(4,1)}), s8[4194304]{0:T(1024)(128)(4,1)S(1)}, s32[]{:S(2)}) async-start(s8[12582912]{0:T(1024)(128)(4,1)} %bitcast.285), calls=%async_computation.12 | async-start | bytes 8388608
  1458.5 42.9 %all-to-all-start.3 = ((f32[4,1,98304]{2,1,0:T(1,128)}), f32[4,1,98304]{2,1,0:T(1,128)S(1)}, u32[]{:S(2)}, u32[]{:S(2)}) async-start(f32[4,1,98304]{2,1,0:T(1,128)} %reshape.298), calls=%async_computation.3 | async-start | bytes 3145728 | tf_op jit(solution)/shard_map/all_to_all | solution.py:168
  1463.0 4.5 collective-permute-start
  1464.3 4.0 collective-permute-start.1
  1469.4 49.2 %collective-permute-start.2 = (f32[3,258,1]{2,1,0:T(8,128)}, f32[3,258,1]{2,1,0:T(8,128)}, u32[]{:S(2)}, u32[]{:S(2)}) collective-permute-start(f32[3,258,1]{2,1,0:T(8,128)} %get-tuple-element.68), channel_id=1, source_target_pairs={{1,0},{2,1},{3,2},{5,4},{6,5},{7,6},{9,8},{10,9},{11,10},{13,12},{... | collective-permute-start | bytes 9296 | tf_op jit(solution)/shard_map/ppermute | solution.py:21
  1470.7 47.9 %collective-permute-start.3 = (f32[3,258,1]{2,1,0:T(8,128)}, f32[3,258,1]{2,1,0:T(8,128)}, u32[]{:S(2)}, u32[]{:S(2)}) collective-permute-start(f32[3,258,1]{2,1,0:T(8,128)} %get-tuple-element.69), channel_id=1, source_target_pairs={{0,1},{1,2},{2,3},{4,5},{5,6},{6,7},{8,9},{9,10},{10,11},{12,13},{... | collective-permute-start | bytes 9296 | tf_op jit(solution)/shard_map/ppermute | solution.py:20
  1522.2 55.1 %copy-start.18 = (f32[1,256,512]{2,1,0:T(8,128)}, f32[1,256,512]{2,1,0:T(8,128)S(1)}, u32[]{:S(2)}) copy-start(f32[1,256,512]{2,1,0:T(8,128)S(1)} %get-tuple-element.13) | copy-start | bytes 1572868
  1522.2 55.1 %copy-start.24 = (f32[1,256,512]{2,1,0:T(8,128)}, f32[1,256,512]{2,1,0:T(8,128)S(1)}, u32[]{:S(2)}) copy-start(f32[1,256,512]{2,1,0:T(8,128)S(1)} %get-tuple-element.12) | copy-start | bytes 1572868
  1522.4 57.1 %copy-start.22 = (f32[1,256,512]{2,1,0:T(8,128)}, f32[1,256,512]{2,1,0:T(8,128)S(1)}, u32[]{:S(2)}) copy-start(f32[1,256,512]{2,1,0:T(8,128)S(1)} %multiply_subtract_fusion.10) | copy-start | bytes 1572868
  2536.1 69.5 %slice-start = ((s8[12582912]{0:T(1024)(128)(4,1)}), s8[4194304]{0:T(1024)(128)(4,1)S(1)}, s32[]{:S(2)}) async-start(s8[12582912]{0:T(1024)(128)(4,1)} %bitcast.283), calls=%async_computation.8 | async-start | bytes 8388608
  2536.1 69.5 %slice-start.1 = ((s8[12582912]{0:T(1024)(128)(4,1)}), s8[4194304]{0:T(1024)(128)(4,1)S(1)}, s32[]{:S(2)}) async-start(s8[12582912]{0:T(1024)(128)(4,1)} %bitcast.283), calls=%async_computation.9 | async-start | bytes 8388608
  2556.2 49.4 %slice-start.2 = ((s8[12582912]{0:T(1024)(128)(4,1)}), s8[4194304]{0:T(1024)(128)(4,1)S(1)}, s32[]{:S(2)}) async-start(s8[12582912]{0:T(1024)(128)(4,1)} %bitcast.283), calls=%async_computation.10 | async-start | bytes 8388608
  2964.7 42.9 %all-to-all-start.7 = ((f32[4,1,98304]{2,1,0:T(1,128)}), f32[4,1,98304]{2,1,0:T(1,128)S(1)}, u32[]{:S(2)}, u32[]{:S(2)}) async-start(f32[4,1,98304]{2,1,0:T(1,128)} %reshape.300), calls=%async_computation.7 | async-start | bytes 3145728 | tf_op jit(solution)/shard_map/all_to_all | solution.py:168
  2969.3 4.5 collective-permute-start.4
  2970.6 4.0 collective-permute-start.5
  2975.6 49.0 %collective-permute-start.6 = (f32[3,258,1]{2,1,0:T(8,128)}, f32[3,258,1]{2,1,0:T(8,128)S(1)}, u32[]{:S(2)}, u32[]{:S(2)}) collective-permute-start(f32[3,258,1]{2,1,0:T(8,128)} %get-tuple-element.66), channel_id=1, source_target_pairs={{1,0},{2,1},{3,2},{5,4},{6,5},{7,6},{9,8},{10,9},{11,10},{13,12},{... | collective-permute-start | bytes 9296 | tf_op jit(solution)/shard_map/ppermute | solution.py:21
  2976.9 47.7 %collective-permute-start.7 = (f32[3,258,1]{2,1,0:T(8,128)}, f32[3,258,1]{2,1,0:T(8,128)}, u32[]{:S(2)}, u32[]{:S(2)}) collective-permute-start(f32[3,258,1]{2,1,0:T(8,128)} %get-tuple-element.67), channel_id=1, source_target_pairs={{0,1},{1,2},{2,3},{4,5},{5,6},{6,7},{8,9},{9,10},{10,11},{12,13},{... | collective-permute-start | bytes 9296 | tf_op jit(solution)/shard_map/ppermute | solution.py:20
  (44 other events, 561.0 us)
where the time goes:
time: 3060 us; the launch traced here: 3030 us
  local copies, waits for them, and re-layouts  956 us (31%)
  other arithmetic  672 us (22%)
  matrix products  654 us (21%)
  blocking collectives  478 us (16%)
  waiting for transfers between devices  229 us (7%)
  starting transfers between devices  41.9 us (1%)
    dot_general x32, matrix products, contract(): return jnp.einsum(form, left, right, precision=lax.Precision.HIGHEST)  654 us
    all_to_all x2, blocking collectives, send_back(): lax.all_to_all(partial_value, ('tx', 'ty'), split_axis=0, concat_axis=1,...  286 us
    neg x18, other arithmetic, turn(): -paired[..., 1]  246 us
    another operation x18, other arithmetic, turn(): jnp.stack([-paired[..., 1], paired[..., 0]], axis=-1).reshape(values.shape)  245 us
    reshape x8, local copies, waits for them, and re-layouts, turn(): jnp.stack([-paired[..., 1], paired[..., 0]], axis=-1).reshape(values.shape)  159 us
    all_to_all x1, blocking collectives, send_out(): lax.all_to_all(spectra, ('tx', 'ty'), split_axis=1, concat_axis=0, tiled=...  141 us
    all_to_all x1, waiting for transfers between devices, send_out(): lax.all_to_all(spectra, ('tx', 'ty'), split_axis=1, concat_axis=0, tiled=...  130 us
    another operation x4, local copies, waits for them, and re-layouts, x_inverse(): shaped = spectra.reshape(second_len, first_len, width)  91.6 us
  transfers between devices with their start and end apart: 12, of which 6 were waited for; matrix products, arithmetic and copies ran while one was open for 1% of the time, Pallas kernels for 0%

commit v1 on v0

v1 whole, which is shorter than its diff:
```python
import functools
import math

import jax
import jax.numpy as jnp
import numpy as np
from jax import lax
from jax.experimental import pallas as pl
from jax.experimental.pallas import tpu as pltpu
from jax.sharding import PartitionSpec as P

DAMPING = 0.3
STIFFNESS = 0.25
TIME_STEP = 0.25
LANES = 128
AXES = ("tx", "ty")


def halves(values):
    high = values.astype(jnp.bfloat16)
    low = (values - high.astype(jnp.float32)).astype(jnp.bfloat16)
    return high, low


def np_halves(values):
    values = np.asarray(values, np.float64)
    high = values.astype(np.float32).astype(jnp.bfloat16)
    low = (values - high.astype(np.float64)).astype(np.float32).astype(jnp.bfloat16)
    return jnp.asarray(high), jnp.asarray(low)


def dot(left, right, dims):
    return lax.dot_general(left, right, (dims, ((), ())), preferred_element_type=jnp.float32)


def dot_3(left, right, dims=((1,), (0,))):
    return (
        dot(left[0], right[0], dims) + dot(left[1], right[0], dims) + dot(left[0], right[1], dims)
    )


NT = ((1,), (1,))


def c_add(a, b):
    if a is None:
        return b
    if b is None:
        return a
    re = a[0] + b[0]
    if a[1] is None or b[1] is None:
        return (re, b[1] if a[1] is None else a[1])
    return (re, a[1] + b[1])


def c_sub(a, b):
    if b is None:
        return a
    re = a[0] - b[0]
    if b[1] is None:
        return (re, a[1])
    return (re, -b[1] if a[1] is None else a[1] - b[1])


def c_turn(a, num, den, sign):
    num %= den
    if a is None or num == 0:
        return a
    re, im = a
    if 4 * num == den:
        return (None, sign * re) if im is None else (-sign * im, sign * re)
    cos, sin = math.cos(2 * math.pi * num / den), sign * math.sin(2 * math.pi * num / den)
    if im is None:
        return (re * cos, re * sin)
    return (re * cos - im * sin, re * sin + im * cos)


def fix(a):
    if a is not None and a[0] is None:
        return (jnp.zeros_like(a[1]), a[1])
    return a


def fft(items, sign, wanted):
    size = len(items)
    if size == 1:
        return {0: items[0]}
    half = size // 2
    result = {}
    even = sorted({k // 2 for k in wanted if k % 2 == 0})
    odd = sorted({k // 2 for k in wanted if k % 2 == 1})
    if even:
        sub = fft([c_add(items[i], items[i + half]) for i in range(half)], sign, even)
        result.update({2 * k: v for k, v in sub.items()})
    if odd:
        parts = [
            fix(c_turn(c_sub(items[i], items[i + half]), i, size, sign)) for i in range(half)
        ]
        result.update({2 * k + 1: v for k, v in fft(parts, sign, odd).items()})
    return result


class Plan:
    def __init__(self, mag_shape, n_tx, n_ty):
        self.n_ty = n_ty
        self.devices = n = n_tx * n_ty
        self.block_x, self.block_y = mag_shape[1:]
        self.rows = self.block_x // n_ty
        self.len_x, self.len_y = 2 * self.block_x * n_tx, 2 * self.block_y * n_ty
        self.slots = self.len_y // 2 // LANES
        self.residues = 2 * self.slots
        self.near = self.len_y // n // self.residues
        self.group = LANES // self.rows
        self.steps = self.slots // self.group
        self.freq = n * 2 * self.near
        self.spread = 2 * n * self.near

    def y_tables(self):
        k1 = np.arange(LANES)
        spot = np.arange(LANES)
        angle = 2 * np.pi * np.outer(k1, spot) / LANES
        cos, sin = np.cos(angle), np.sin(angle)

        def rows(re_re, re_im, im_re, im_im):
            full = np.stack(
                [np.concatenate([re_re, re_im], 1), np.concatenate([im_re, im_im], 1)]
            )
            full = full.reshape(2, self.devices, self.near, 2 * LANES)
            return full.transpose(1, 0, 2, 3).reshape(self.freq, 2 * LANES)

        plain = rows(cos, sin, -sin, cos)
        mixed = rows(-sin, cos, -cos, -sin)
        slot = np.arange(self.slots)
        turn = 2 * np.pi * np.outer(slot, spot) / self.len_y
        turn_cos = np.tile(np.cos(turn), 2).reshape(self.steps, 1, self.group * 2 * LANES)
        turn_sin = np.tile(np.sin(turn), 2).reshape(self.steps, 1, self.group * 2 * LANES)
        late = 2 * np.pi * np.outer(k1 + 0.5, spot) / LANES
        low = (k1 < LANES // 2)[:, None]
        zero = np.zeros_like(cos)
        im_first = np.where(low, -sin, 0)
        im_first[0] = np.cos(np.pi * spot)
        first = rows(
            np.where(low, cos, zero),
            np.where(low, zero, np.cos(late)),
            im_first,
            np.where(low, zero, -np.sin(late)),
        )
        return plain, mixed, turn_cos, turn_sin, first

    def y_matrices(self):
        plain, mixed, turn_cos, turn_sin, first = (
            jnp.asarray(t, jnp.float32) for t in self.y_tables()
        )
        plain = jnp.concatenate([plain] * self.group, axis=1)[None]
        mixed = jnp.concatenate([mixed] * self.group, axis=1)[None]
        full = plain * turn_cos + mixed * turn_sin
        first = jnp.pad(first, ((0, 0), (0, (self.group - 1) * 2 * LANES)))[None]
        shape = (self.steps, 1, self.group * 2 * LANES)
        at_first = (lax.broadcasted_iota(jnp.int32, shape, 0) == 0) & (
            lax.broadcasted_iota(jnp.int32, shape, 2) < 2 * LANES
        )
        return jnp.where(at_first, first, full)

    def x_first(self):
        n = self.devices
        angle = 2 * np.pi * np.outer(np.arange(2 * n), np.arange(n)) / (2 * n)
        cos, sin = np.cos(angle), np.sin(angle)
        table = np.stack([np.stack([cos, sin], -1), np.stack([-sin, cos], -1)])
        full = np.einsum("orsi,fg->orfsig", table, np.eye(self.near))
        return full.reshape(2 * self.spread, self.freq)

    def x_turn(self):
        angle = -2 * np.pi * np.outer(np.arange(2 * self.devices), np.arange(self.rows))
        angle = np.repeat(angle / self.len_x, self.near, axis=0)
        angle = np.tile(angle, (1, self.group))
        return np.stack([np.cos(angle), np.sin(angle)]).astype(np.float32)

    def x_second(self):
        span = np.arange(self.rows)
        angle = 2 * np.pi * np.outer(span, span) / self.rows
        cos, sin = np.cos(angle), np.sin(angle)
        table = np.stack([np.stack([cos, -sin], 1), np.stack([sin, cos], 1)])
        full = np.einsum("ixok,qp->iqxopk", table, np.eye(self.group))
        return full.reshape(2 * LANES, 2 * LANES)


def y_forward_kernel(plan, rows_ref, high_ref, low_ref, out_ref, z_high, z_low):
    step = pl.program_id(0)
    chunk = 16
    per = plan.rows // chunk
    blocks = plan.block_y // LANES

    @pl.when(step == 0)
    def _():
        if plan.group > 1:
            z_high[...] = jnp.zeros_like(z_high)
            z_low[...] = jnp.zeros_like(z_low)

        def one(index, carry):
            comp = index // per
            start = pl.multiple_of((index % per) * chunk, chunk)
            items = []
            for block in range(plan.slots):
                lane = block % blocks * LANES
                items.append(
                    (
                        rows_ref[
                            block // blocks, comp, pl.ds(start, chunk), lane : lane + LANES
                        ],
                        None,
                    )
                )
            items += [None] * plan.slots
            parts = fft(items, -1, list(range(plan.slots + 1)))
            for slot in range(plan.slots):
                pair = (parts[0][0], parts[plan.slots][0]) if slot == 0 else parts[slot]
                place, inner = slot // plan.group, slot % plan.group
                row = pl.multiple_of(comp * LANES + inner * plan.rows + start, chunk)
                for half in range(2):
                    lane = inner * 2 * LANES + half * LANES
                    high, low = halves(pair[half])
                    z_high[place, pl.ds(row, chunk), lane : lane + LANES] = high
                    z_low[place, pl.ds(row, chunk), lane : lane + LANES] = low
            return carry

        lax.fori_loop(0, 3 * per, one, 0)

    left = (high_ref[0], low_ref[0])
    out_ref[...] = dot_3(left, (z_high[step], z_low[step]), NT)


def y_forward(plan, rows, high, low):
    wide = 3 * LANES
    deep = plan.group * 2 * LANES
    matrix = pl.BlockSpec((1, plan.freq, deep), lambda i: (i, 0, 0))
    return pl.pallas_call(
        functools.partial(y_forward_kernel, plan),
        grid=(plan.steps,),
        in_specs=[
            pl.BlockSpec(rows.shape, lambda i: (0, 0, 0, 0)),
            matrix,
            matrix,
        ],
        out_specs=pl.BlockSpec((plan.freq, wide), lambda i: (0, i)),
        out_shape=jax.ShapeDtypeStruct((plan.freq, wide * plan.steps), jnp.float32),
        scratch_shapes=[
            pltpu.VMEM((plan.steps, wide, deep), jnp.bfloat16),
            pltpu.VMEM((plan.steps, wide, deep), jnp.bfloat16),
        ],
        compiler_params=pltpu.CompilerParams(vmem_limit_bytes=50 * 2**20),
        cost_estimate=pl.CostEstimate(
            flops=6 * plan.freq * wide * plan.steps * deep,
            bytes_accessed=10 * 2**20,
            transcendentals=0,
        ),
        name="y_forward",
    )(rows, high, low)


def x_kernel(
    plan,
    data_ref,
    gain_ref,
    shift_ref,
    mirror_ref,
    one_high,
    one_low,
    back_high,
    back_low,
    two_high,
    two_low,
    turn_ref,
    out_ref,
    field_ref,
):
    one = (one_high[...], one_low[...])
    two = (two_high[...], two_low[...])
    turn_re, turn_im = turn_ref[0], turn_ref[1]
    size = plan.spread

    def cut(comp):
        return slice(comp * LANES, (comp + 1) * LANES)

    def spectrum(data):
        section = dot_3(one, halves(data))
        result = []
        for comp in range(3):
            re, im = section[:size, cut(comp)], section[size:, cut(comp)]
            turned = jnp.concatenate(
                [re * turn_re - im * turn_im, re * turn_im + im * turn_re], axis=1
            )
            result.append(dot_3(halves(turned), two))
        return result

    def apply(gain, parts):
        result = []
        for comp in range(3):
            wide = [jnp.concatenate([gain(i)] * 2, axis=1) for i in ((0, 3), (3, 1), (2,))[comp]]
            if comp == 2:
                result.append(wide[0] * parts[2])
            else:
                result.append(wide[0] * parts[0] + wide[1] * parts[1])
        return result

    data = data_ref[...]
    parts = spectrum(data)
    for comp, value in enumerate(apply(lambda i: gain_ref[i, 0], parts)):
        field_ref[comp] = value

    @pl.when(pl.program_id(0) == 0)
    def _():
        row = lax.broadcasted_iota(jnp.int32, (plan.freq, 1), 0)
        sign = jnp.where(row // plan.near % 2 == 0, 1.0, -1.0)
        other = spectrum(data * sign)
        added = apply(lambda i: shift_ref[i], parts)
        flipped = apply(lambda i: mirror_ref[i], other)
        for comp in range(3):
            field_ref[comp] += added[comp] + flipped[comp]

    re_list, im_list = [], []
    for comp in range(3):
        value = dot_3(halves(field_ref[comp]), two, NT)
        re, im = value[:, :LANES], value[:, LANES:]
        re_list.append(re * turn_re + im * turn_im)
        im_list.append(im * turn_re - re * turn_im)
    section = jnp.concatenate(
        [jnp.concatenate(re_list, axis=1), jnp.concatenate(im_list, axis=1)], axis=0
    )
    out_ref[...] = dot_3((back_high[...], back_low[...]), halves(section))


def x_stage(plan, data, gains, tables):
    gain, shift, mirror = gains
    wide = 3 * LANES
    lane_block = pl.BlockSpec((plan.freq, wide), lambda i: (0, i))

    def whole(array):
        return pl.BlockSpec(array.shape, lambda i: (0,) * array.ndim)

    return pl.pallas_call(
        functools.partial(x_kernel, plan),
        grid=(plan.steps,),
        in_specs=[
            lane_block,
            pl.BlockSpec((4, 1, plan.spread, LANES), lambda i: (0, i, 0, 0)),
            whole(shift),
            whole(mirror),
            *[whole(t) for t in tables],
        ],
        out_specs=lane_block,
        out_shape=jax.ShapeDtypeStruct(data.shape, jnp.float32),
        scratch_shapes=[pltpu.VMEM((3, plan.spread, 2 * LANES), jnp.float32)],
        compiler_params=pltpu.CompilerParams(vmem_limit_bytes=50 * 2**20),
        cost_estimate=pl.CostEstimate(
            flops=24 * plan.freq * wide * plan.steps * 2 * plan.spread,
            bytes_accessed=12 * 2**20,
            transcendentals=0,
        ),
        name="x_stage",
    )(data, gain, shift, mirror, *tables)


def y_inverse_kernel(plan, data_ref, high_ref, low_ref, turn_ref, out_ref, inner_ref, sum_ref):
    step = pl.program_id(0)
    value = dot_3((high_ref[0], low_ref[0]), halves(data_ref[...]))
    deep = 2 * LANES
    lane = lax.broadcasted_iota(jnp.int32, (1, LANES), 1)
    for comp in range(3):
        mixed = value[:deep, comp * LANES : (comp + 1) * LANES]
        for inner in range(1, plan.group):
            mixed = jnp.where(
                lane // plan.rows == inner,
                value[inner * deep : (inner + 1) * deep, comp * LANES : (comp + 1) * LANES],
                mixed,
            )
        inner_ref[comp, step] = mixed

    @pl.when(step == plan.steps - 1)
    def _():
        chunk = 8
        blocks = plan.block_y // LANES

        def one_comp(comp, carry):
            def one(index, carry):
                start = pl.multiple_of(index * chunk, chunk)
                items = [
                    (
                        inner_ref[comp, place, pl.ds(start, chunk), :],
                        inner_ref[comp, place, pl.ds(LANES + start, chunk), :],
                    )
                    for place in range(plan.steps)
                ]
                odd = jnp.where(lane < plan.rows, items[0][1], 0.0)
                period = 2 * plan.steps
                parts = fft(items + [None] * plan.steps, 1, list(range(period)))
                for block in range(plan.slots):
                    re, im = parts[block % period]
                    total = re * turn_ref[0, block : block + 1, :]
                    total = total - im * turn_ref[1, block : block + 1, :]
                    total = total + odd if block % 2 == 0 else total - odd
                    shift = LANES // 2
                    while shift >= plan.rows:
                        total = total + pltpu.roll(total, shift, 1)
                        shift //= 2
                    sum_ref[block, pl.ds(start, chunk), :] = total
                return carry

            lax.fori_loop(0, LANES // chunk, one, 0)
            for block in range(plan.slots):
                first = block % blocks * LANES
                out_ref[block // blocks, comp, :, first : first + LANES] = sum_ref[block].T[
                    : plan.rows
                ]
            return carry

        lax.fori_loop(0, 3, one_comp, 0)


def y_inverse(plan, data, high, low):
    wide = 3 * LANES
    deep = plan.group * 2 * LANES
    matrix = pl.BlockSpec((1, deep, plan.freq), lambda i: (i, 0, 0))
    shape = (plan.n_ty, 3, plan.rows, plan.block_y)
    inner = np.arange(LANES) // plan.rows
    angle = 2 * np.pi * np.outer(np.arange(plan.slots), inner) / plan.residues
    turn = jnp.asarray(np.stack([np.cos(angle), np.sin(angle)]), jnp.float32)
    return pl.pallas_call(
        functools.partial(y_inverse_kernel, plan),
        grid=(plan.steps,),
        in_specs=[
            pl.BlockSpec((plan.freq, wide), lambda i: (0, i)),
            matrix,
            matrix,
            pl.BlockSpec(turn.shape, lambda i: (0, 0, 0)),
        ],
        out_specs=pl.BlockSpec(shape, lambda i: (0, 0, 0, 0)),
        out_shape=jax.ShapeDtypeStruct(shape, jnp.float32),
        scratch_shapes=[
            pltpu.VMEM((3, plan.steps, 2 * LANES, LANES), jnp.float32),
            pltpu.VMEM((plan.slots, LANES, LANES), jnp.float32),
        ],
        compiler_params=pltpu.CompilerParams(vmem_limit_bytes=50 * 2**20),
        cost_estimate=pl.CostEstimate(
            flops=6 * plan.freq * wide * plan.steps * deep,
            bytes_accessed=10 * 2**20,
            transcendentals=0,
        ),
        name="y_inverse",
    )(data, high, low, turn)


def kernel_gains(plan, kernel):
    n, near, slots = plan.devices, plan.near, plan.slots
    me = lax.axis_index(AXES)
    scale = 2.0 / (plan.len_x * plan.len_y)
    kx = np.arange(plan.len_x)
    wave_x = jnp.asarray(2 * STIFFNESS * np.cos(2 * np.pi * kx / plan.len_x), jnp.float32)
    diagonal = jnp.asarray([1.0, 1.0, 1.0, 0.0], jnp.float32)

    nyquist = lax.ppermute(kernel[:, 0, :], AXES, [(n // 2, 0)])
    split = kernel.reshape(4, near, plan.residues, plan.len_x)
    first = jnp.where(me < n // 2, split[:, :, :1], split[:, :, slots : slots + 1])
    chosen = jnp.concatenate([first, split[:, :, 1:slots]], axis=2)
    slot = lax.broadcasted_iota(jnp.int32, (near, slots), 1)
    slot = jnp.where((slot == 0) & (me >= n // 2), slots, slot)
    ky = (me * near + lax.broadcasted_iota(jnp.int32, (near, slots), 0)) * plan.residues + slot
    wave_y = 2 * STIFFNESS * jnp.cos(ky.astype(jnp.float32) * (2 * math.pi / plan.len_y))
    wave = wave_x[None, None, :] + wave_y[:, :, None]
    gain = (diagonal[:, None, None, None] * wave[None] - chosen) * scale

    def arrange(array, count_near, count_slots):
        group = min(plan.group, count_slots)
        shaped = array.reshape(4, count_near, count_slots // group, group, plan.rows, 2 * n)
        moved = shaped.transpose(0, 2, 5, 1, 3, 4)
        return moved.reshape(4, count_slots // group, 2 * n * count_near, group * plan.rows)

    zero_row = (diagonal[:, None] * (wave_x + 2 * STIFFNESS)[None] - kernel[:, 0, :]) * scale
    last_row = (diagonal[:, None] * (wave_x - 2 * STIFFNESS)[None] - nyquist) * scale
    shift = jnp.where(me == 0, 0.25 * (zero_row + last_row) - zero_row, 0.0)
    mirror = jnp.where(me == 0, 0.25 * (zero_row - last_row), 0.0)

    def place(row):
        small = row.reshape(4, plan.rows, 2 * n).transpose(0, 2, 1)[:, :, None, :]
        small = jnp.pad(small, ((0, 0), (0, 0), (0, near - 1), (0, LANES - plan.rows)))
        return small.reshape(4, plan.spread, LANES)

    return arrange(gain, near, slots), place(shift), place(mirror)


def cross(left, right):
    return jnp.stack(
        [
            left[1] * right[2] - left[2] * right[1],
            left[2] * right[0] - left[0] * right[2],
            left[0] * right[1] - left[1] * right[0],
        ]
    )


def exchange(values, axes):
    return lax.all_to_all(values, axes, split_axis=0, concat_axis=0, tiled=True)


def body(mag, occupancy, kernel_spectrum):
    plan = Plan(mag.shape, lax.axis_size("tx"), lax.axis_size("ty"))
    occ = occupancy.astype(jnp.float32)
    start = mag * occ[None]
    matrix = plan.y_matrices()
    rounded = lax.reduce_precision(matrix, 8, 7)
    high, low = rounded.astype(jnp.bfloat16), (matrix - rounded).astype(jnp.bfloat16)
    high_back, low_back = jnp.swapaxes(high, 1, 2), jnp.swapaxes(low, 1, 2)
    one = plan.x_first()
    tables = (
        *np_halves(one),
        *np_halves(one.T),
        *np_halves(plan.x_second()),
        jnp.asarray(plan.x_turn()),
    )
    gains = kernel_gains(plan, kernel_spectrum)
    sent_shape = (plan.devices, 2 * plan.near, 3 * plan.slots * plan.rows)
    flat_shape = (plan.freq, sent_shape[2])

    def effective(field):
        shaped = field.reshape(3, plan.n_ty, plan.rows, plan.block_y).transpose(1, 0, 2, 3)
        rows = exchange(shaped, "ty")
        spectra = y_forward(plan, rows, high, low)
        columns = exchange(spectra.reshape(sent_shape), AXES).reshape(flat_shape)
        product = x_stage(plan, columns, gains, tables)
        returned = exchange(product.reshape(sent_shape), AXES).reshape(flat_shape)
        spatial = exchange(y_inverse(plan, returned, high_back, low_back), "ty")
        return spatial.transpose(1, 0, 2, 3).reshape(field.shape)

    def rate(field):
        torque = cross(field, effective(field))
        return -(torque + DAMPING * cross(field, torque)) / (1.0 + DAMPING * DAMPING)

    def normal(vector):
        return vector / jnp.sqrt(jnp.sum(vector * vector, axis=0) + 1.0 - occ)[None]

    first = rate(start)
    middle = normal(start + TIME_STEP * first)
    second = rate(middle)
    second = second - jnp.sum(second * start, axis=0)[None] * start
    mean_rate = 0.5 * (first + second)
    mag_next = normal(start + TIME_STEP * mean_rate)
    return (mag_next, mean_rate)


def solution(mesh):
    return jax.shard_map(
        body,
        mesh=mesh,
        in_specs=(P(None, "tx", "ty"), P("tx", "ty"), P(None, ("tx", "ty"), None)),
        out_specs=(P(None, "tx", "ty"), P(None, "tx", "ty")),
        check_vma=False,
    )
```

time: 3060 us -> 577 us (0.19)
  local copies, waits for them, and re-layouts: 956 us -> 48.6 us
  matrix products: 654 us -> 0 us
  other arithmetic: 672 us -> 34.9 us
  blocking collectives: 478 us -> 270 us
  waiting for transfers between devices: 229 us -> 115 us
  Pallas kernels: 0 us -> 88 us
    dot_general x32 -> x0, matrix products: 654 us -> none  [contract(): return jnp.einsum(form, left, right, precision=lax.Precision.HIGHEST)]
    another operation x16 -> x0, local copies, waits for them, and re-layouts: 301 us -> none  [the longest x4 91.6 us: x_inverse(): shaped = spectra.reshape(second_len, first_len, width)]
    another operation x22 -> x0, other arithmetic: 268 us -> none  [the longest x18 245 us: turn(): jnp.stack([-paired[..., 1], paired[..., 0]], axis=-1).reshape(values.shape)]
    neg x20 -> x0, other arithmetic: 267 us -> none  [the longest x18 246 us: turn(): -paired[..., 1]]
    reshape x14 -> x7, local copies, waits for them, and re-layouts: 223 us -> 11.5 us  [the longest x1 8.88 us: arrange(): moved.reshape(4, count_slots // group, 2 * n * count_near, group * plan.r...]
    all_to_all x4 -> x5, blocking collectives: 478 us -> 270 us  [exchange(): return lax.all_to_all(values, axes, split_axis=0, concat_axis=0, tiled=True)]
    sub x8 -> x0, local copies, waits for them, and re-layouts: 171 us -> none  [the longest x2 47.4 us: x_forward(): contract('abz,ac->cbz', shaped, cos_one)]
    all_to_all x4 -> x3, waiting for transfers between devices: 228 us -> 115 us  [exchange(): return lax.all_to_all(values, axes, split_axis=0, concat_axis=0, tiled=True)]
  transfers between devices with their start and end apart: 12 -> 4, of which waited for: 6 -> 3; matrix products, arithmetic and copies ran while one was open for 1% -> 10% of each run, Pallas kernels for 0% -> 0%
where the time goes in v1:
time: 577 us; the launch traced here: 574 us
  blocking collectives  270 us (47%)
  waiting for transfers between devices  115 us (20%)
  Pallas kernels  88 us (15%)
  local copies, waits for them, and re-layouts  48.6 us (8%)
  other arithmetic  34.9 us (6%)
  starting transfers between devices  16.8 us (3%)
    all_to_all x5, blocking collectives, exchange(): return lax.all_to_all(values, axes, split_axis=0, concat_axis=0, tiled=True)  270 us
    all_to_all x3, waiting for transfers between devices, exchange(): return lax.all_to_all(values, axes, split_axis=0, concat_axis=0, tiled=True)  115 us
    pallas_call x2, Pallas kernels, x_stage(): pl.pallas_call(functools.partial(x_kernel, plan), grid=(plan.steps,), in_...  39.4 us
    pallas_call x2, Pallas kernels, y_inverse(): pl.pallas_call(functools.partial(y_inverse_kernel, plan), grid=(plan.step...  27.2 us
    pallas_call x2, Pallas kernels, y_forward(): pl.pallas_call(functools.partial(y_forward_kernel, plan), grid=(plan.step...  21.4 us
    all_to_all x3, starting transfers between devices, exchange(): return lax.all_to_all(values, axes, split_axis=0, concat_axis=0, tiled=True)  15.3 us
    transpose x1, local copies, waits for them, and re-layouts, arrange(): moved = shaped.transpose(0, 2, 5, 1, 3, 4)  13.2 us
  transfers between devices with their start and end apart: 4, of which 3 were waited for; matrix products, arithmetic and copies ran while one was open for 10% of the time, Pallas kernels for 0%

profile of v1, /device:TPU:0, one launch (start us, length us, event | category | flops | bytes accessed | tf_op | source)
XLA Modules:
  0.0 574.3 jit_solution(12575715022119934790)
XLA Ops:
  5.2 6.5 %all-to-all-start = ((f32[4,3,64,512]{3,2,1,0:T(8,128)}), f32[4,3,64,512]{3,2,1,0:T(8,128)}, u32[]{:S(2)}, u32[]{:S(2)}) async-start(f32[4,3,64,512]{3,2,1,0:T(8,128)} %bitcast.50), calls=%async_computation | async-start | bytes 3145728 | tf_op jit(solution)/shard_map/all_to_all | solution.py:501
  12.4 3.5 fusion
  15.9 32.9 %all-to-all-done.rows_ref = f32[4,3,64,512]{3,2,1,0:T(8,128)} async-done(((f32[4,3,64,512]{3,2,1,0:T(8,128)}), f32[4,3,64,512]{3,2,1,0:T(8,128)}, u32[]{:S(2)}, u32[]{:S(2)}) %all-to-all-start) | async-done | bytes 1572896 | tf_op jit(solution)/shard_map/all_to_all | solution.py:501
  48.8 11.0 %y_forward.2 = f32[256,3072]{1,0:T(8,128)} custom-call(f32[4,3,64,512]{3,2,1,0:T(8,128)} %all-to-all-done.rows_ref, bf16[8,256,512]{2,1,0:T(8,128)(2,1)S(1)} %get-tuple-element.17.high_ref, bf16[8,256,512]{2,1,0:T(8,128)(2,1)} %get-tuple-element.16.low_ref), custom_call_target="tpu_custom_call" | custom-call | flops 2415919104 | bytes 10485760 | tf_op jit(solution)/shard_map/y_forward/pallas_call | solution.py:236
  59.8 3.8 all-to-all-start.1
  66.2 3.2 slice.98
  74.6 7.8 %concatenate.14 = f32[4,4,8,2,64,64]{5,4,3,2,1,0:T(8,128)} reshape(f32[4,4,16,4096]{3,2,1,0:T(8,128)} %pad_maximum_fusion) | data formatting | bytes 8388608 | tf_op jit(solution)/shard_map/concatenate | solution.py:463
  83.1 8.7 %multiply_bitcast_fusion = f32[4,8,64,4,2,64]{2,5,4,1,3,0:T(8,128)} fusion(f32[4,4,8,2,64,64]{5,4,3,2,1,0:T(8,128)} %concatenate.14, f32[4,8,2,64,64]{4,3,2,1,0:T(8,128)S(1)} %broadcast_add_fusion, f32[4]{0:T(128)S(1)} %copy-done.29), kind=kLoop, calls=%fused_computation | loop fusion | flops 3145728 | bytes 9437200 | tf_op jit(solution)/shard_map/transpose | solution.py:474
  91.8 13.2 %copy.24 = f32[4,8,64,4,2,64]{5,4,3,2,1,0:T(2,128)} copy(f32[4,8,64,4,2,64]{2,5,4,1,3,0:T(8,128)} %multiply_bitcast_fusion) | data formatting | bytes 8388608 | tf_op jit(solution)/shard_map/transpose | solution.py:474
  105.0 8.9 %reshape.190.gain_ref = f32[4,8,256,128]{3,2,1,0:T(8,128)} reshape(f32[4,8,64,4,2,64]{5,4,3,2,1,0:T(2,128)} %copy.24) | data formatting | bytes 8388608 | tf_op jit(solution)/shard_map/reshape | solution.py:475
  116.3 17.3 %all-to-all-done.1 = f32[32,8,3072]{2,1,0:T(8,128)} async-done(((f32[32,8,3072]{2,1,0:T(8,128)}), f32[32,8,3072]{2,1,0:T(8,128)}, u32[]{:S(2)}, u32[]{:S(2)}) %all-to-all-start.1) | async-done | bytes 3145760 | tf_op jit(solution)/shard_map/all_to_all | solution.py:501
  138.3 19.7 %x_stage.2 = f32[256,3072]{1,0:T(8,128)} custom-call(f32[256,3072]{1,0:T(8,128)} %bitcast.3.data_ref, f32[4,8,256,128]{3,2,1,0:T(8,128)} %reshape.190.gain_ref, f32[4,256,128]{2,1,0:T(8,128)S(1)} %bitcast.44, f32[4,256,128]{2,1,0:T(8,128)S(1)} %bitcast.46, bf16[512,256]{1,0:T(8,128)(2,1)S(1)} %copy-done.9, bf16[512,256]{1,0:T(8,128)(2,1)S(1)} %copy-done.7, ...), custom_call_target="tpu_custom_call" | custom-call | flops 9663676416 | bytes 12582912 | tf_op jit(solution)/shard_map/x_stage/pallas_call | solution.py:340
  158.0 5.0 all-to-all-start.2
  163.0 5.2 fusion.1
  168.1 64.8 %all-to-all-done.2 = f32[32,8,3072]{2,1,0:T(8,128)} async-done(((f32[32,8,3072]{2,1,0:T(8,128)}), f32[32,8,3072]{2,1,0:T(8,128)}, u32[]{:S(2)}, u32[]{:S(2)}) %all-to-all-start.2) | async-done | bytes 3145760 | tf_op jit(solution)/shard_map/all_to_all | solution.py:501
  234.5 13.6 %y_inverse.2 = f32[4,3,64,512]{3,2,1,0:T(8,128)S(1)} custom-call(f32[256,3072]{1,0:T(8,128)} %bitcast.13.data_ref, bf16[8,512,256]{2,1,0:T(8,128)(2,1)S(1)} %copy-done, bf16[8,512,256]{2,1,0:T(8,128)(2,1)} %get-tuple-element.14.low_ref, f32[2,16,128]{2,1,0:T(8,128)S(1)} %copy-done.14), custom_call_target="tpu_custom_call" | custom-call | flops 2415919104 | bytes 10485760 | tf_op jit(solution)/shard_map/y_inverse/pallas_call | solution.py:427
  248.1 41.4 %all_to_all.40 = f32[4,3,64,512]{3,2,1,0:T(8,128)S(1)} all-to-all(f32[4,3,64,512]{3,2,1,0:T(8,128)S(1)} %y_inverse.2), channel_id=1, replica_groups=mesh['tx'=8,'ty'=4] {'ty'}, dimensions={0} | all-to-all | bytes 3145728 | tf_op jit(solution)/shard_map/all_to_all | solution.py:501
  295.3 39.2 %all_to_all.41.rows_ref = f32[4,3,64,512]{3,2,1,0:T(8,128)S(1)} all-to-all(f32[4,3,64,512]{3,2,1,0:T(8,128)S(1)} %bitcast.53), channel_id=1, replica_groups=mesh['tx'=8,'ty'=4] {'ty'}, dimensions={0} | all-to-all | bytes 3145728 | tf_op jit(solution)/shard_map/all_to_all | solution.py:501
  334.5 10.4 %y_forward.3 = f32[256,3072]{1,0:T(8,128)} custom-call(f32[4,3,64,512]{3,2,1,0:T(8,128)S(1)} %all_to_all.41.rows_ref, bf16[8,256,512]{2,1,0:T(8,128)(2,1)S(1)} %get-tuple-element.17.high_ref, bf16[8,256,512]{2,1,0:T(8,128)(2,1)} %get-tuple-element.16.low_ref), custom_call_target="tpu_custom_call" | custom-call | flops 2415919104 | bytes 10485760 | tf_op jit(solution)/shard_map/y_forward/pallas_call | solution.py:236
  344.9 73.5 %all_to_all.42 = f32[32,8,3072]{2,1,0:T(8,128)} all-to-all(f32[32,8,3072]{2,1,0:T(8,128)} %bitcast.67), channel_id=1, replica_groups=mesh['tx'=8,'ty'=4] {'tx','ty'}, dimensions={0} | all-to-all | bytes 6291456 | tf_op jit(solution)/shard_map/all_to_all | solution.py:501
  418.5 19.7 %x_stage.3 = f32[256,3072]{1,0:T(8,128)} custom-call(f32[256,3072]{1,0:T(8,128)} %bitcast.64, f32[4,8,256,128]{3,2,1,0:T(8,128)} %reshape.190.gain_ref, f32[4,256,128]{2,1,0:T(8,128)S(1)} %bitcast.45, f32[4,256,128]{2,1,0:T(8,128)S(1)} %bitcast.47, bf16[512,256]{1,0:T(8,128)(2,1)S(1)} %copy-done.10, bf16[512,256]{1,0:T(8,128)(2,1)S(1)} %copy-done.8, ...), custom_call_target="tpu_custom_call" | custom-call | flops 9663676416 | bytes 12582912 | tf_op jit(solution)/shard_map/x_stage/pallas_call | solution.py:340
  438.2 74.5 %all_to_all.43 = f32[32,8,3072]{2,1,0:T(8,128)} all-to-all(f32[32,8,3072]{2,1,0:T(8,128)} %bitcast.65), channel_id=1, replica_groups=mesh['tx'=8,'ty'=4] {'tx','ty'}, dimensions={0} | all-to-all | bytes 6291456 | tf_op jit(solution)/shard_map/all_to_all | solution.py:501
  512.7 13.6 %y_inverse.3 = f32[4,3,64,512]{3,2,1,0:T(8,128)S(1)} custom-call(f32[256,3072]{1,0:T(8,128)} %bitcast.66, bf16[8,512,256]{2,1,0:T(8,128)(2,1)S(1)} %copy-done.1, bf16[8,512,256]{2,1,0:T(8,128)(2,1)} %get-tuple-element.14.low_ref, f32[2,16,128]{2,1,0:T(8,128)S(1)} %copy-done.14), custom_call_target="tpu_custom_call" | custom-call | flops 2415919104 | bytes 10485760 | tf_op jit(solution)/shard_map/y_inverse/pallas_call | solution.py:427
  526.3 41.5 %all_to_all.44 = f32[4,3,64,512]{3,2,1,0:T(8,128)S(1)} all-to-all(f32[4,3,64,512]{3,2,1,0:T(8,128)S(1)} %y_inverse.3), channel_id=1, replica_groups=mesh['tx'=8,'ty'=4] {'ty'}, dimensions={0} | all-to-all | bytes 3145728 | tf_op jit(solution)/shard_map/all_to_all | solution.py:501
  (101 shorter events, 34.4 us)
Async XLA Ops:
  1.7 1.8 copy-start.18
  3.6 1.7 copy-start.16
  5.2 7.2 %copy-start.21 = (f32[256,512]{1,0:T(8,128)S(1)}, f32[256,512]{1,0:T(8,128)}, u32[]{:S(2)}) copy-start(f32[256,512]{1,0:T(8,128)} %constant.107) | copy-start | bytes 1572868
  5.2 7.2 %copy-start.22 = (f32[256,512]{1,0:T(8,128)S(1)}, f32[256,512]{1,0:T(8,128)}, u32[]{:S(2)}) copy-start(f32[256,512]{1,0:T(8,128)} %constant.105) | copy-start | bytes 1572868
  5.2 7.2 %copy-start.23 = (f32[8,512]{1,0:T(8,128)S(1)}, f32[8,512]{1,0:T(8,128)}, u32[]{:S(2)}) copy-start(f32[8,512]{1,0:T(8,128)} %constant.108) | copy-start | bytes 49156
  5.2 7.2 %copy-start.24 = (f32[8,512]{1,0:T(8,128)S(1)}, f32[8,512]{1,0:T(8,128)}, u32[]{:S(2)}) copy-start(f32[8,512]{1,0:T(8,128)} %constant.106) | copy-start | bytes 49156
  5.2 43.6 %all-to-all-start = ((f32[4,3,64,512]{3,2,1,0:T(8,128)}), f32[4,3,64,512]{3,2,1,0:T(8,128)}, u32[]{:S(2)}, u32[]{:S(2)}) async-start(f32[4,3,64,512]{3,2,1,0:T(8,128)} %bitcast.50), calls=%async_computation | async-start | bytes 3145728 | tf_op jit(solution)/shard_map/all_to_all | solution.py:501
  59.8 73.8 %all-to-all-start.1 = ((f32[32,8,3072]{2,1,0:T(8,128)}), f32[32,8,3072]{2,1,0:T(8,128)}, u32[]{:S(2)}, u32[]{:S(2)}) async-start(f32[32,8,3072]{2,1,0:T(8,128)} %bitcast.62), calls=%async_computation.1 | async-start | bytes 6291456 | tf_op jit(solution)/shard_map/all_to_all | solution.py:501
  64.7 49.2 %collective-permute-start = (f32[4,4096]{1,0:T(4,128)S(1)}, f32[4,4096]{1,0:T(4,128)S(1)}, u32[]{:S(2)}, u32[]{:S(2)}) collective-permute-start(f32[4,4096]{1,0:T(4,128)S(1)} %bitcast.74), channel_id=1, source_target_pairs={{16,0}} | collective-permute-start | bytes 196616 | tf_op jit(solution)/shard_map/ppermute | solution.py:460
  74.6 8.0 %copy-start.26 = (f32[64,64]{1,0:T(8,128)S(1)}, f32[64,64]{1,0:T(8,128)}, u32[]{:S(2)}) copy-start(f32[64,64]{1,0:T(8,128)} %constant.109) | copy-start | bytes 49156
  105.0 8.9 %copy-start.27 = (f32[4096]{0:T(1024)S(1)}, f32[4096]{0:T(1024)}, u32[]{:S(2)}) copy-start(f32[4096]{0:T(1024)} %constant.111) | copy-start | bytes 49156
  105.0 8.9 %copy-start.28 = (f32[4096]{0:T(1024)S(1)}, f32[4096]{0:T(1024)}, u32[]{:S(2)}) copy-start(f32[4096]{0:T(1024)} %constant.110) | copy-start | bytes 49156
  113.9 19.6 %copy-start.2 = (f32[2,256,128]{2,1,0:T(8,128)S(1)}, f32[2,256,128]{2,1,0:T(8,128)}, u32[]{:S(2)}) copy-start(f32[2,256,128]{2,1,0:T(8,128)} %constant.94.clone.turn_ref) | copy-start | bytes 786436
  113.9 19.6 %copy-start.11 = (bf16[256,256]{1,0:T(8,128)(2,1)S(1)}, bf16[256,256]{1,0:T(8,128)(2,1)}, u32[]{:S(2)}) copy-start(bf16[256,256]{1,0:T(8,128)(2,1)} %constant.93.clone.two_low) | copy-start | bytes 393220
  158.0 74.9 %all-to-all-start.2 = ((f32[32,8,3072]{2,1,0:T(8,128)}), f32[32,8,3072]{2,1,0:T(8,128)}, u32[]{:S(2)}, u32[]{:S(2)}) async-start(f32[32,8,3072]{2,1,0:T(8,128)} %bitcast.63), calls=%async_computation.2 | async-start | bytes 6291456 | tf_op jit(solution)/shard_map/all_to_all | solution.py:501
  162.9 70.0 %copy-start.14 = (f32[2,16,128]{2,1,0:T(8,128)S(1)}, f32[2,16,128]{2,1,0:T(8,128)}, u32[]{:S(2)}) copy-start(f32[2,16,128]{2,1,0:T(8,128)} %constant.97.clone.turn_ref) | copy-start | bytes 49156
  232.9 1.6 copy-start
  291.7 1.5 copy-start.19
  344.9 73.6 %copy-start.4 = (bf16[256,512]{1,0:T(8,128)(2,1)S(1)}, bf16[256,512]{1,0:T(8,128)(2,1)}, u32[]{:S(2)}) copy-start(bf16[256,512]{1,0:T(8,128)(2,1)} %constant.91.clone.back_low) | copy-start | bytes 786436
  344.9 73.6 %copy-start.6 = (bf16[256,512]{1,0:T(8,128)(2,1)S(1)}, bf16[256,512]{1,0:T(8,128)(2,1)}, u32[]{:S(2)}) copy-start(bf16[256,512]{1,0:T(8,128)(2,1)} %constant.90.clone.back_high) | copy-start | bytes 786436
  344.9 73.6 %copy-start.8 = (bf16[512,256]{1,0:T(8,128)(2,1)S(1)}, bf16[512,256]{1,0:T(8,128)(2,1)}, u32[]{:S(2)}) copy-start(bf16[512,256]{1,0:T(8,128)(2,1)} %constant.89.clone.one_low) | copy-start | bytes 786436
  344.9 73.6 %copy-start.10 = (bf16[512,256]{1,0:T(8,128)(2,1)S(1)}, bf16[512,256]{1,0:T(8,128)(2,1)}, u32[]{:S(2)}) copy-start(bf16[512,256]{1,0:T(8,128)(2,1)} %constant.88.clone.one_high) | copy-start | bytes 786436
  344.9 73.6 %copy-start.13 = (bf16[256,256]{1,0:T(8,128)(2,1)S(1)}, bf16[256,256]{1,0:T(8,128)(2,1)}, u32[]{:S(2)}) copy-start(bf16[256,256]{1,0:T(8,128)(2,1)} %constant.92.clone.two_high) | copy-start | bytes 393220
  438.2 74.5 %copy-start.1 = (bf16[8,512,256]{2,1,0:T(8,128)(2,1)S(1)}, bf16[8,512,256]{2,1,0:T(8,128)(2,1)}, u32[]{:S(2)}) copy-start(bf16[8,512,256]{2,1,0:T(8,128)(2,1)} %get-tuple-element.15.high_ref) | copy-start | bytes 6291460
  (10 other events, 9.8 us)

commit v2 on v1

--- a/solution.py
+++ b/solution.py
@@ -184,7 +184,7 @@
         return full.reshape(2 * LANES, 2 * LANES)
 
 
-def y_forward_kernel(plan, rows_ref, high_ref, low_ref, out_ref, z_high, z_low):
+def y_forward_kernel(plan, place_ref, rows_ref, high_ref, low_ref, out_ref, z_high, z_low):
     step = pl.program_id(0)
     chunk = 16
     per = plan.rows // chunk
@@ -205,7 +205,10 @@
                 items.append(
                     (
                         rows_ref[
-                            block // blocks, comp, pl.ds(start, chunk), lane : lane + LANES
+                            lax.bitwise_xor(block // blocks, place_ref[0]),
+                            comp,
+                            pl.ds(start, chunk),
+                            lane : lane + LANES,
                         ],
                         None,
                     )
@@ -223,20 +226,21 @@
                     z_low[place, pl.ds(row, chunk), lane : lane + LANES] = low
             return carry
 
-        lax.fori_loop(0, 3 * per, one, 0)
+        lax.fori_loop(0, rows_ref.shape[1] * per, one, 0)
 
     left = (high_ref[0], low_ref[0])
     out_ref[...] = dot_3(left, (z_high[step], z_low[step]), NT)
 
 
-def y_forward(plan, rows, high, low):
-    wide = 3 * LANES
+def y_forward(plan, place, rows, high, low):
+    wide = rows.shape[1] * LANES
     deep = plan.group * 2 * LANES
     matrix = pl.BlockSpec((1, plan.freq, deep), lambda i: (i, 0, 0))
     return pl.pallas_call(
         functools.partial(y_forward_kernel, plan),
         grid=(plan.steps,),
         in_specs=[
+            pl.BlockSpec(memory_space=pltpu.SMEM),
             pl.BlockSpec(rows.shape, lambda i: (0, 0, 0, 0)),
             matrix,
             matrix,
@@ -254,7 +258,7 @@
             transcendentals=0,
         ),
         name="y_forward",
-    )(rows, high, low)
+    )(place, rows, high, low)
 
 
 def x_kernel(
@@ -277,6 +281,7 @@
     two = (two_high[...], two_low[...])
     turn_re, turn_im = turn_ref[0], turn_ref[1]
     size = plan.spread
+    count = field_ref.shape[0]
 
     def cut(comp):
         return slice(comp * LANES, (comp + 1) * LANES)
@@ -284,7 +289,7 @@
     def spectrum(data):
         section = dot_3(one, halves(data))
         result = []
-        for comp in range(3):
+        for comp in range(count):
             re, im = section[:size, cut(comp)], section[size:, cut(comp)]
             turned = jnp.concatenate(
                 [re * turn_re - im * turn_im, re * turn_im + im * turn_re], axis=1
@@ -293,14 +298,13 @@
         return result
 
     def apply(gain, parts):
-        result = []
-        for comp in range(3):
-            wide = [jnp.concatenate([gain(i)] * 2, axis=1) for i in ((0, 3), (3, 1), (2,))[comp]]
-            if comp == 2:
-                result.append(wide[0] * parts[2])
-            else:
-                result.append(wide[0] * parts[0] + wide[1] * parts[1])
-        return result
+        wide = [jnp.concatenate([gain(i)] * 2, axis=1) for i in range(2 * count - 1)]
+        if count == 1:
+            return [wide[0] * parts[0]]
+        return [
+            wide[0] * parts[0] + wide[2] * parts[1],
+            wide[2] * parts[0] + wide[1] * parts[1],
+        ]
 
     data = data_ref[...]
     parts = spectrum(data)
@@ -314,11 +318,11 @@
         other = spectrum(data * sign)
         added = apply(lambda i: shift_ref[i], parts)
         flipped = apply(lambda i: mirror_ref[i], other)
-        for comp in range(3):
+        for comp in range(count):
             field_ref[comp] += added[comp] + flipped[comp]
 
     re_list, im_list = [], []
-    for comp in range(3):
+    for comp in range(count):
         value = dot_3(halves(field_ref[comp]), two, NT)
         re, im = value[:, :LANES], value[:, LANES:]
         re_list.append(re * turn_re + im * turn_im)
@@ -331,7 +335,8 @@
 
 def x_stage(plan, data, gains, tables):
     gain, shift, mirror = gains
-    wide = 3 * LANES
+    count = (gain.shape[0] + 1) // 2
+    wide = count * LANES
     lane_block = pl.BlockSpec((plan.freq, wide), lambda i: (0, i))
 
     def whole(array):
@@ -342,14 +347,14 @@
         grid=(plan.steps,),
         in_specs=[
             lane_block,
-            pl.BlockSpec((4, 1, plan.spread, LANES), lambda i: (0, i, 0, 0)),
+            pl.BlockSpec((gain.shape[0], 1, plan.spread, LANES), lambda i: (0, i, 0, 0)),
             whole(shift),
             whole(mirror),
             *[whole(t) for t in tables],
         ],
         out_specs=lane_block,
         out_shape=jax.ShapeDtypeStruct(data.shape, jnp.float32),
-        scratch_shapes=[pltpu.VMEM((3, plan.spread, 2 * LANES), jnp.float32)],
+        scratch_shapes=[pltpu.VMEM((count, plan.spread, 2 * LANES), jnp.float32)],
         compiler_params=pltpu.CompilerParams(vmem_limit_bytes=50 * 2**20),
         cost_estimate=pl.CostEstimate(
             flops=24 * plan.freq * wide * plan.steps * 2 * plan.spread,
@@ -360,12 +365,13 @@
     )(data, gain, shift, mirror, *tables)
 
 
-def y_inverse_kernel(plan, data_ref, high_ref, low_ref, turn_ref, out_ref, inner_ref, sum_ref):
+def y_inverse_kernel(plan, place_ref, data_ref, high_ref, low_ref, turn_ref, out_ref, inner_ref, sum_ref):
     step = pl.program_id(0)
     value = dot_3((high_ref[0], low_ref[0]), halves(data_ref[...]))
     deep = 2 * LANES
     lane = lax.broadcasted_iota(jnp.int32, (1, LANES), 1)
-    for comp in range(3):
+    count = out_ref.shape[1]
+    for comp in range(count):
         mixed = value[:deep, comp * LANES : (comp + 1) * LANES]
         for inner in range(1, plan.group):
             mixed = jnp.where(
@@ -408,19 +414,19 @@
             lax.fori_loop(0, LANES // chunk, one, 0)
             for block in range(plan.slots):
                 first = block % blocks * LANES
-                out_ref[block // blocks, comp, :, first : first + LANES] = sum_ref[block].T[
-                    : plan.rows
-                ]
+                target = lax.bitwise_xor(block // blocks, place_ref[0])
+                out_ref[target, comp, :, first : first + LANES] = sum_ref[block].T[: plan.rows]
             return carry
 
-        lax.fori_loop(0, 3, one_comp, 0)
-
-
-def y_inverse(plan, data, high, low):
-    wide = 3 * LANES
+        lax.fori_loop(0, count, one_comp, 0)
+
+
+def y_inverse(plan, place, data, high, low):
+    wide = data.shape[1] // plan.steps
+    count = wide // LANES
     deep = plan.group * 2 * LANES
     matrix = pl.BlockSpec((1, deep, plan.freq), lambda i: (i, 0, 0))
-    shape = (plan.n_ty, 3, plan.rows, plan.block_y)
+    shape = (plan.n_ty, count, plan.rows, plan.block_y)
     inner = np.arange(LANES) // plan.rows
     angle = 2 * np.pi * np.outer(np.arange(plan.slots), inner) / plan.residues
     turn = jnp.asarray(np.stack([np.cos(angle), np.sin(angle)]), jnp.float32)
@@ -428,6 +434,7 @@
         functools.partial(y_inverse_kernel, plan),
         grid=(plan.steps,),
         in_specs=[
+            pl.BlockSpec(memory_space=pltpu.SMEM),
             pl.BlockSpec((plan.freq, wide), lambda i: (0, i)),
             matrix,
             matrix,
@@ -436,7 +443,7 @@
         out_specs=pl.BlockSpec(shape, lambda i: (0, 0, 0, 0)),
         out_shape=jax.ShapeDtypeStruct(shape, jnp.float32),
         scratch_shapes=[
-            pltpu.VMEM((3, plan.steps, 2 * LANES, LANES), jnp.float32),
+            pltpu.VMEM((count, plan.steps, 2 * LANES, LANES), jnp.float32),
             pltpu.VMEM((plan.slots, LANES, LANES), jnp.float32),
         ],
         compiler_params=pltpu.CompilerParams(vmem_limit_bytes=50 * 2**20),
@@ -446,19 +453,20 @@
             transcendentals=0,
         ),
         name="y_inverse",
-    )(data, high, low, turn)
-
-
-def kernel_gains(plan, kernel):
+    )(place, data, high, low, turn)
+
+
+def kernel_gains(plan, kernel, diagonal):
     n, near, slots = plan.devices, plan.near, plan.slots
     me = lax.axis_index(AXES)
     scale = 2.0 / (plan.len_x * plan.len_y)
     kx = np.arange(plan.len_x)
     wave_x = jnp.asarray(2 * STIFFNESS * np.cos(2 * np.pi * kx / plan.len_x), jnp.float32)
-    diagonal = jnp.asarray([1.0, 1.0, 1.0, 0.0], jnp.float32)
+    count = kernel.shape[0]
+    diagonal = jnp.asarray(diagonal, jnp.float32)
 
     nyquist = lax.ppermute(kernel[:, 0, :], AXES, [(n // 2, 0)])
-    split = kernel.reshape(4, near, plan.residues, plan.len_x)
+    split = kernel.reshape(count, near, plan.residues, plan.len_x)
     first = jnp.where(me < n // 2, split[:, :, :1], split[:, :, slots : slots + 1])
     chosen = jnp.concatenate([first, split[:, :, 1:slots]], axis=2)
     slot = lax.broadcasted_iota(jnp.int32, (near, slots), 1)
@@ -470,9 +478,9 @@
 
     def arrange(array, count_near, count_slots):
         group = min(plan.group, count_slots)
-        shaped = array.reshape(4, count_near, count_slots // group, group, plan.rows, 2 * n)
+        shaped = array.reshape(count, count_near, count_slots // group, group, plan.rows, 2 * n)
         moved = shaped.transpose(0, 2, 5, 1, 3, 4)
-        return moved.reshape(4, count_slots // group, 2 * n * count_near, group * plan.rows)
+        return moved.reshape(count, count_slots // group, 2 * n * count_near, group * plan.rows)
 
     zero_row = (diagonal[:, None] * (wave_x + 2 * STIFFNESS)[None] - kernel[:, 0, :]) * scale
     last_row = (diagonal[:, None] * (wave_x - 2 * STIFFNESS)[None] - nyquist) * scale
@@ -480,11 +488,12 @@
     mirror = jnp.where(me == 0, 0.25 * (zero_row - last_row), 0.0)
 
     def place(row):
-        small = row.reshape(4, plan.rows, 2 * n).transpose(0, 2, 1)[:, :, None, :]
+        small = row.reshape(count, plan.rows, 2 * n).transpose(0, 2, 1)[:, :, None, :]
         small = jnp.pad(small, ((0, 0), (0, 0), (0, near - 1), (0, LANES - plan.rows)))
-        return small.reshape(4, plan.spread, LANES)
-
-    return arrange(gain, near, slots), place(shift), place(mirror)
+        return small.reshape(count, plan.spread, LANES)
+
+    arrays = (arrange(gain, near, slots), place(shift), place(mirror))
+    return arrays
 
 
 def cross(left, right):
@@ -495,6 +504,11 @@
             left[0] * right[1] - left[1] * right[0],
         ]
     )
+
+
+def swap(values, axis, offset):
+    size = lax.axis_size(axis)
+    return lax.ppermute(values, axis, [(i, i ^ offset) for i in range(size)])
 
 
 def exchange(values, axes):
@@ -516,19 +530,57 @@
         *np_halves(plan.x_second()),
         jnp.asarray(plan.x_turn()),
     )
-    gains = kernel_gains(plan, kernel_spectrum)
-    sent_shape = (plan.devices, 2 * plan.near, 3 * plan.slots * plan.rows)
-    flat_shape = (plan.freq, sent_shape[2])
+    gain_b = kernel_gains(plan, kernel_spectrum[2:3], (1.0,))
+    paired = jnp.concatenate([kernel_spectrum[:2], kernel_spectrum[3:]])
+    gain_a = kernel_gains(plan, paired, (1.0, 1.0, 0.0))
+
+    def sent(array):
+        return array.reshape(plan.devices, 2 * plan.near, array.shape[1])
+
+    def flat(array):
+        return array.reshape(plan.freq, array.shape[2])
+
+    here = lax.axis_index("ty")
+    place = here.reshape(1)
+
+    def start_row(offset):
+        return (here ^ offset) * plan.rows
+
+    def gather_rows(field):
+        size = (field.shape[0], plan.rows, plan.block_y)
+        pieces = []
+        for offset in range(plan.n_ty):
+            piece = lax.dynamic_slice(field, (0, start_row(offset), 0), size)
+            pieces.append(swap(piece, "ty", offset) if offset else piece)
+        return jnp.stack(pieces)
+
+    def return_rows(spatial):
+        count = spatial.shape[1]
+        field = jnp.zeros((count, plan.block_x, plan.block_y), jnp.float32)
+        for offset in range(plan.n_ty):
+            piece = swap(spatial[offset], "ty", offset) if offset else spatial[0]
+            field = lax.dynamic_update_slice(field, piece, (0, start_row(offset), 0))
+        return field
 
     def effective(field):
-        shaped = field.reshape(3, plan.n_ty, plan.rows, plan.block_y).transpose(1, 0, 2, 3)
-        rows = exchange(shaped, "ty")
-        spectra = y_forward(plan, rows, high, low)
-        columns = exchange(spectra.reshape(sent_shape), AXES).reshape(flat_shape)
-        product = x_stage(plan, columns, gains, tables)
-        returned = exchange(product.reshape(sent_shape), AXES).reshape(flat_shape)
-        spatial = exchange(y_inverse(plan, returned, high_back, low_back), "ty")
-        return spatial.transpose(1, 0, 2, 3).reshape(field.shape)
+        rows_a = gather_rows(field[:2])
+        rows_b = gather_rows(field[2:])
+        spectra_a = sent(y_forward(plan, place, rows_a, high, low))
+        columns_a = exchange(spectra_a, AXES)
+        spectra_b = sent(y_forward(plan, place, rows_b, high, low))
+        columns_a, spectra_b = lax.optimization_barrier((columns_a, spectra_b))
+        columns_b = exchange(spectra_b, AXES)
+        product_a = sent(x_stage(plan, flat(columns_a), gain_a, tables))
+        product_a, columns_b = lax.optimization_barrier((product_a, columns_b))
+        returned_a = exchange(product_a, AXES)
+        product_b = sent(x_stage(plan, flat(columns_b), gain_b, tables))
+        returned_a, product_b = lax.optimization_barrier((returned_a, product_b))
+        returned_b = exchange(product_b, AXES)
+        spatial_a = y_inverse(plan, place, flat(returned_a), high_back, low_back)
+        field_a = return_rows(spatial_a)
+        spatial_b = y_inverse(plan, place, flat(returned_b), high_back, low_back)
+        field_b = return_rows(spatial_b)
+        return jnp.concatenate([field_a, field_b])
 
     def rate(field):
         torque = cross(field, effective(field))

time: 577 us -> 567 us (0.983)
  blocking collectives: 270 us -> 0 us
  waiting for transfers between devices: 115 us -> 208 us
  starting transfers between devices: 16.8 us -> 92.2 us
  Pallas kernels: 88 us -> 140 us
  local copies, waits for them, and re-layouts: 48.6 us -> 78.2 us
  other arithmetic: 34.9 us -> 44 us
    all_to_all x5 -> x0, blocking collectives: 270 us -> none  [exchange(): return lax.all_to_all(values, axes, split_axis=0, concat_axis=0, tiled=True)]
    ppermute x0 -> x24, waiting for transfers between devices: none -> 162 us  [swap(): return lax.ppermute(values, axis, [(i, i ^ offset) for i in range(size)])]
    all_to_all x3 -> x8, waiting for transfers between devices: 115 us -> 45.9 us  [exchange(): return lax.all_to_all(values, axes, split_axis=0, concat_axis=0, tiled=True)]
    ppermute x0 -> x24, starting transfers between devices: none -> 43.8 us  [swap(): return lax.ppermute(values, axis, [(i, i ^ offset) for i in range(size)])]
    all_to_all x3 -> x8, starting transfers between devices: 15.3 us -> 45.9 us  [exchange(): return lax.all_to_all(values, axes, split_axis=0, concat_axis=0, tiled=True)]
    pallas_call x2 -> x4, Pallas kernels: 39.4 us -> 69.6 us  [x_stage(): pl.pallas_call(functools.partial(x_kernel, plan), grid=(plan.steps,), in_...]
    unnamed x61 -> x169, local copies, waits for them, and re-layouts: 10.5 us -> 28.7 us
    pallas_call x2 -> x4, Pallas kernels: 21.4 us -> 33.3 us  [y_forward(): pl.pallas_call(functools.partial(y_forward_kernel, plan), grid=(plan.step...]
  transfers between devices with their start and end apart: 4 -> 34, of which waited for: 3 -> 17; matrix products, arithmetic and copies ran while one was open for 10% -> 15% of each run, Pallas kernels for 0% -> 20%
where the time goes in v2:
time: 567 us; the launch traced here: 564 us
  waiting for transfers between devices  208 us (37%)
  Pallas kernels  140 us (25%)
  starting transfers between devices  92.2 us (16%)
  local copies, waits for them, and re-layouts  78.2 us (14%)
  other arithmetic  44 us (8%)
    ppermute x24, waiting for transfers between devices, swap(): return lax.ppermute(values, axis, [(i, i ^ offset) for i in range(size)])  162 us
    pallas_call x4, Pallas kernels, x_stage(): pl.pallas_call(functools.partial(x_kernel, plan), grid=(plan.steps,), in_...  69.6 us
    all_to_all x8, starting transfers between devices, exchange(): return lax.all_to_all(values, axes, split_axis=0, concat_axis=0, tiled=True)  45.9 us
    all_to_all x8, waiting for transfers between devices, exchange(): return lax.all_to_all(values, axes, split_axis=0, concat_axis=0, tiled=True)  45.9 us
    ppermute x24, starting transfers between devices, swap(): return lax.ppermute(values, axis, [(i, i ^ offset) for i in range(size)])  43.8 us
    pallas_call x4, Pallas kernels, y_inverse(): pl.pallas_call(functools.partial(y_inverse_kernel, plan), grid=(plan.step...  36.9 us
    pallas_call x4, Pallas kernels, y_forward(): pl.pallas_call(functools.partial(y_forward_kernel, plan), grid=(plan.step...  33.3 us
    unnamed x169, local copies, waits for them, and re-layouts  28.7 us
  transfers between devices with their start and end apart: 34, of which 17 were waited for; matrix products, arithmetic and copies ran while one was open for 15% of the time, Pallas kernels for 20%

profile of v2, /device:TPU:0, one launch (start us, length us, event | category | flops | bytes accessed | tf_op | source)
XLA Modules:
  0.0 563.8 jit_solution(13649327739046159843)
XLA Ops:
  16.8 10.1 %collective-permute-done = f32[2,64,512]{2,1,0:T(8,128)S(1)} collective-permute-done((f32[2,64,512]{2,1,0:T(8,128)S(1)}, f32[2,64,512]{2,1,0:T(8,128)S(1)}, u32[]{:S(2)}, u32[]{:S(2)}) %collective-permute-start) | collective-permute-done | bytes 262176 | tf_op jit(solution)/shard_map/ppermute | solution.py:511
  26.9 8.5 %collective-permute-done.1 = f32[2,64,512]{2,1,0:T(8,128)S(1)} collective-permute-done((f32[2,64,512]{2,1,0:T(8,128)S(1)}, f32[2,64,512]{2,1,0:T(8,128)S(1)}, u32[]{:S(2)}, u32[]{:S(2)}) %collective-permute-start.1) | collective-permute-done | bytes 262176 | tf_op jit(solution)/shard_map/ppermute | solution.py:511
  35.5 9.1 %y_forward.4 = f32[256,2048]{1,0:T(8,128)} custom-call(s32[1]{0:T(128)} %bitcast.1.place_ref, f32[4,2,64,512]{3,2,1,0:T(8,128)S(1)} %pad_maximum_fusion.2.rows_ref, bf16[8,256,512]{2,1,0:T(8,128)(2,1)} %get-tuple-element.45.high_ref, bf16[8,256,512]{2,1,0:T(8,128)(2,1)} %get-tuple-element.44.low_ref), custom_call_target="tpu_custom_call" | custom-call | flops 1610612736 | bytes 10485760 | tf_op jit(solution)/shard_map/y_forward/pallas_call | solution.py:239
  44.5 9.0 %all-to-all-start = ((f32[32,8,2048]{2,1,0:T(8,128)}), f32[32,8,2048]{2,1,0:T(8,128)}, u32[]{:S(2)}, u32[]{:S(2)}) async-start(f32[32,8,2048]{2,1,0:T(8,128)} %bitcast.6), calls=%async_computation | async-start | bytes 4194304 | tf_op jit(solution)/shard_map/all_to_all | solution.py:515
  84.8 15.6 %all-to-all-done = f32[32,8,2048]{2,1,0:T(8,128)} async-done(((f32[32,8,2048]{2,1,0:T(8,128)}), f32[32,8,2048]{2,1,0:T(8,128)}, u32[]{:S(2)}, u32[]{:S(2)}) %all-to-all-start) | async-done | bytes 2097184 | tf_op jit(solution)/shard_map/all_to_all | solution.py:515
  112.1 10.2 %copy.27 = f32[3,8,64,4,2,64]{5,4,3,2,1,0:T(2,128)} copy(f32[3,8,64,4,2,64]{2,5,4,1,3,0:T(8,128)} %multiply_bitcast_fusion) | data formatting | bytes 6291456 | tf_op jit(solution)/shard_map/transpose | solution.py:482
  131.3 20.2 %x_stage.4 = f32[256,2048]{1,0:T(8,128)} custom-call(f32[256,2048]{1,0:T(8,128)} %bitcast.12.data_ref, f32[3,8,256,128]{3,2,1,0:T(8,128)} %reshape.257.gain_ref, f32[3,256,128]{2,1,0:T(8,128)S(1)} %bitcast.284, f32[3,256,128]{2,1,0:T(8,128)S(1)} %bitcast.286, bf16[512,256]{1,0:T(8,128)(2,1)S(1)} %copy-done.13, bf16[512,256]{1,0:T(8,128)(2,1)S(1)} %copy-done.17, ...), custom_call_target="tpu_custom_call" | custom-call | flops 6442450944 | bytes 12582912 | tf_op jit(solution)/shard_map/x_stage/pallas_call | solution.py:345
  193.3 14.6 %x_stage.5 = f32[256,1024]{1,0:T(8,128)S(1)} custom-call(f32[256,1024]{1,0:T(8,128)S(1)} %bitcast.280, f32[1,8,256,128]{3,2,1,0:T(8,128)} %reshape.265.gain_ref, f32[1,256,128]{2,1,0:T(8,128)S(1)} %bitcast.288, f32[1,256,128]{2,1,0:T(8,128)S(1)} %bitcast.290, bf16[512,256]{1,0:T(8,128)(2,1)S(1)} %copy-done.14, bf16[512,256]{1,0:T(8,128)(2,1)S(1)} %copy-done.18, ...), custom_call_target="tpu_custom_call" | custom-call | flops 3221225472 | bytes 12582912 | tf_op jit(solution)/shard_map/x_stage/pallas_call | solution.py:345
  220.8 10.4 %y_inverse.5 = f32[4,2,64,512]{3,2,1,0:T(8,128)S(1)} custom-call(s32[1]{0:T(128)} %bitcast.1.place_ref, f32[256,2048]{1,0:T(8,128)S(1)} %bitcast.276, bf16[8,512,256]{2,1,0:T(8,128)(2,1)} %get-tuple-element.43.high_ref, bf16[8,512,256]{2,1,0:T(8,128)(2,1)} %get-tuple-element.42.low_ref, f32[2,16,128]{2,1,0:T(8,128)S(1)} %copy-done.8), custom_call_target="tpu_custom_call" | custom-call | flops 1610612736 | bytes 10485760 | tf_op jit(solution)/shard_map/y_inverse/pallas_call | solution.py:433
  235.9 8.5 %collective-permute-done.11 = f32[2,64,512]{2,1,0:T(8,128)S(1)} collective-permute-done((f32[2,64,512]{2,1,0:T(8,128)S(1)}, f32[2,64,512]{2,1,0:T(8,128)S(1)}, u32[]{:S(2)}, u32[]{:S(2)}) %collective-permute-start.11) | collective-permute-done | bytes 262176 | tf_op jit(solution)/shard_map/ppermute | solution.py:511
  244.4 14.6 %collective-permute-done.12 = f32[2,64,512]{2,1,0:T(8,128)S(1)} collective-permute-done((f32[2,64,512]{2,1,0:T(8,128)S(1)}, f32[2,64,512]{2,1,0:T(8,128)S(1)}, u32[]{:S(2)}, u32[]{:S(2)}) %collective-permute-start.12) | collective-permute-done | bytes 262176 | tf_op jit(solution)/shard_map/ppermute | solution.py:511
  261.1 8.0 %y_inverse.4 = f32[4,1,64,512]{3,2,1,0:T(8,128)S(1)} custom-call(s32[1]{0:T(128)} %bitcast.1.place_ref, f32[256,1024]{1,0:T(8,128)S(1)} %bitcast.278, bf16[8,512,256]{2,1,0:T(8,128)(2,1)S(1)} %copy-done.2, bf16[8,512,256]{2,1,0:T(8,128)(2,1)} %get-tuple-element.42.low_ref, f32[2,16,128]{2,1,0:T(8,128)S(1)} %copy-done.8), custom_call_target="tpu_custom_call" | custom-call | flops 805306368 | bytes 10485760 | tf_op jit(solution)/shard_map/y_inverse/pallas_call | solution.py:433
  279.2 8.0 %collective-permute-done.9 = f32[1,64,512]{2,1,0:T(8,128)S(1)} collective-permute-done((f32[1,64,512]{2,1,0:T(8,128)S(1)}, f32[1,64,512]{2,1,0:T(8,128)S(1)}, u32[]{:S(2)}, u32[]{:S(2)}) %collective-permute-start.9) | collective-permute-done | bytes 131104 | tf_op jit(solution)/shard_map/ppermute | solution.py:511
  304.0 11.9 %collective-permute-done.15 = f32[2,64,512]{2,1,0:T(8,128)S(1)} collective-permute-done((f32[2,64,512]{2,1,0:T(8,128)S(1)}, f32[2,64,512]{2,1,0:T(8,128)S(1)}, u32[]{:S(2)}, u32[]{:S(2)}) %collective-permute-start.15) | collective-permute-done | bytes 262176 | tf_op jit(solution)/shard_map/ppermute | solution.py:511
  316.0 9.1 %y_forward.6 = f32[256,2048]{1,0:T(8,128)} custom-call(s32[1]{0:T(128)} %bitcast.1.place_ref, f32[4,2,64,512]{3,2,1,0:T(8,128)S(1)} %pad_maximum_fusion.4.rows_ref, bf16[8,256,512]{2,1,0:T(8,128)(2,1)} %get-tuple-element.45.high_ref, bf16[8,256,512]{2,1,0:T(8,128)(2,1)} %get-tuple-element.44.low_ref), custom_call_target="tpu_custom_call" | custom-call | flops 1610612736 | bytes 10485760 | tf_op jit(solution)/shard_map/y_forward/pallas_call | solution.py:239
  336.1 33.2 %collective-permute-done.17 = f32[1,64,512]{2,1,0:T(8,128)S(1)} collective-permute-done((f32[1,64,512]{2,1,0:T(8,128)S(1)}, f32[1,64,512]{2,1,0:T(8,128)S(1)}, u32[]{:S(2)}, u32[]{:S(2)}) %collective-permute-start.17) | collective-permute-done | bytes 131104 | tf_op jit(solution)/shard_map/ppermute | solution.py:511
  369.3 20.0 %collective-permute-done.18 = f32[1,64,512]{2,1,0:T(8,128)S(1)} collective-permute-done((f32[1,64,512]{2,1,0:T(8,128)S(1)}, f32[1,64,512]{2,1,0:T(8,128)S(1)}, u32[]{:S(2)}, u32[]{:S(2)}) %collective-permute-start.18) | collective-permute-done | bytes 131104 | tf_op jit(solution)/shard_map/ppermute | solution.py:511
  401.9 20.2 %x_stage.6 = f32[256,2048]{1,0:T(8,128)} custom-call(f32[256,2048]{1,0:T(8,128)} %bitcast.67.data_ref, f32[3,8,256,128]{3,2,1,0:T(8,128)} %reshape.257.gain_ref, f32[3,256,128]{2,1,0:T(8,128)S(1)} %bitcast.285, f32[3,256,128]{2,1,0:T(8,128)S(1)} %bitcast.287, bf16[512,256]{1,0:T(8,128)(2,1)S(1)} %copy-done.15, bf16[512,256]{1,0:T(8,128)(2,1)S(1)} %copy-done.19, ...), custom_call_target="tpu_custom_call" | custom-call | flops 6442450944 | bytes 12582912 | tf_op jit(solution)/shard_map/x_stage/pallas_call | solution.py:345
  437.0 14.6 %x_stage.7 = f32[256,1024]{1,0:T(8,128)S(1)} custom-call(f32[256,1024]{1,0:T(8,128)S(1)} %bitcast.283, f32[1,8,256,128]{3,2,1,0:T(8,128)} %reshape.265.gain_ref, f32[1,256,128]{2,1,0:T(8,128)S(1)} %bitcast.289, f32[1,256,128]{2,1,0:T(8,128)S(1)} %bitcast.291, bf16[512,256]{1,0:T(8,128)(2,1)S(1)} %copy-done.16, bf16[512,256]{1,0:T(8,128)(2,1)S(1)} %copy-done.20, ...), custom_call_target="tpu_custom_call" | custom-call | flops 3221225472 | bytes 12582912 | tf_op jit(solution)/shard_map/x_stage/pallas_call | solution.py:345
  452.5 25.7 %all-to-all-done.6 = f32[32,8,2048]{2,1,0:T(8,128)S(1)} async-done(((f32[32,8,2048]{2,1,0:T(8,128)}), f32[32,8,2048]{2,1,0:T(8,128)S(1)}, u32[]{:S(2)}, u32[]{:S(2)}) %all-to-all-start.6) | async-done | bytes 2097184 | tf_op jit(solution)/shard_map/all_to_all | solution.py:515
  483.0 10.4 %y_inverse.7 = f32[4,2,64,512]{3,2,1,0:T(8,128)S(1)} custom-call(s32[1]{0:T(128)} %bitcast.1.place_ref, f32[256,2048]{1,0:T(8,128)S(1)} %bitcast.277, bf16[8,512,256]{2,1,0:T(8,128)(2,1)} %get-tuple-element.43.high_ref, bf16[8,512,256]{2,1,0:T(8,128)(2,1)} %get-tuple-element.42.low_ref, f32[2,16,128]{2,1,0:T(8,128)S(1)} %copy-done.8), custom_call_target="tpu_custom_call" | custom-call | flops 1610612736 | bytes 10485760 | tf_op jit(solution)/shard_map/y_inverse/pallas_call | solution.py:433
  498.1 9.6 %collective-permute-done.23 = f32[2,64,512]{2,1,0:T(8,128)S(1)} collective-permute-done((f32[2,64,512]{2,1,0:T(8,128)S(1)}, f32[2,64,512]{2,1,0:T(8,128)S(1)}, u32[]{:S(2)}, u32[]{:S(2)}) %collective-permute-start.23) | collective-permute-done | bytes 262176 | tf_op jit(solution)/shard_map/ppermute | solution.py:511
  507.7 18.6 %collective-permute-done.24 = f32[2,64,512]{2,1,0:T(8,128)S(1)} collective-permute-done((f32[2,64,512]{2,1,0:T(8,128)S(1)}, f32[2,64,512]{2,1,0:T(8,128)S(1)}, u32[]{:S(2)}, u32[]{:S(2)}) %collective-permute-start.24) | collective-permute-done | bytes 262176 | tf_op jit(solution)/shard_map/ppermute | solution.py:511
  528.5 8.0 %y_inverse.6 = f32[4,1,64,512]{3,2,1,0:T(8,128)S(1)} custom-call(s32[1]{0:T(128)} %bitcast.1.place_ref, f32[256,1024]{1,0:T(8,128)S(1)} %bitcast.279, bf16[8,512,256]{2,1,0:T(8,128)(2,1)S(1)} %copy-done.3, bf16[8,512,256]{2,1,0:T(8,128)(2,1)} %get-tuple-element.42.low_ref, f32[2,16,128]{2,1,0:T(8,128)S(1)} %copy-done.8), custom_call_target="tpu_custom_call" | custom-call | flops 805306368 | bytes 10485760 | tf_op jit(solution)/shard_map/y_inverse/pallas_call | solution.py:433
  (320 shorter events, 233.8 us)
Async XLA Ops:
  3.7 73.5 %collective-permute-start.5 = (f32[1,64,512]{2,1,0:T(8,128)S(1)}, f32[1,64,512]{2,1,0:T(8,128)S(1)}, u32[]{:S(2)}, u32[]{:S(2)}) collective-permute-start(f32[1,64,512]{2,1,0:T(8,128)S(1)} %get-tuple-element.71), channel_id=1, source_target_pairs={{0,3},{1,2},{2,1},{3,0},{4,7},{5,6},{6,5},{7,4},{8,11},{9,10},{10,... | collective-permute-start | bytes 393224 | tf_op jit(solution)/shard_map/ppermute | solution.py:511
  8.9 68.3 %collective-permute-start.3 = (f32[1,64,512]{2,1,0:T(8,128)S(1)}, f32[1,64,512]{2,1,0:T(8,128)S(1)}, u32[]{:S(2)}, u32[]{:S(2)}) collective-permute-start(f32[1,64,512]{2,1,0:T(8,128)S(1)} %get-tuple-element.73), channel_id=1, source_target_pairs={{0,1},{1,0},{2,3},{3,2},{4,5},{5,4},{6,7},{7,6},{8,9},{9,8},{10,11... | collective-permute-start | bytes 393224 | tf_op jit(solution)/shard_map/ppermute | solution.py:511
  11.2 24.2 %collective-permute-start.1 = (f32[2,64,512]{2,1,0:T(8,128)S(1)}, f32[2,64,512]{2,1,0:T(8,128)S(1)}, u32[]{:S(2)}, u32[]{:S(2)}) collective-permute-start(f32[2,64,512]{2,1,0:T(8,128)S(1)} %get-tuple-element.58), channel_id=1, source_target_pairs={{0,2},{1,3},{2,0},{3,1},{4,6},{5,7},{6,4},{7,5},{8,10},{9,11},{10,... | collective-permute-start | bytes 786440 | tf_op jit(solution)/shard_map/ppermute | solution.py:511
  11.2 24.2 %collective-permute-start.2 = (f32[2,64,512]{2,1,0:T(8,128)S(1)}, f32[2,64,512]{2,1,0:T(8,128)S(1)}, u32[]{:S(2)}, u32[]{:S(2)}) collective-permute-start(f32[2,64,512]{2,1,0:T(8,128)S(1)} %get-tuple-element.57), channel_id=1, source_target_pairs={{0,3},{1,2},{2,1},{3,0},{4,7},{5,6},{6,5},{7,4},{8,11},{9,10},{10,... | collective-permute-start | bytes 786440 | tf_op jit(solution)/shard_map/ppermute | solution.py:511
  26.9 50.3 %collective-permute-start.4 = (f32[1,64,512]{2,1,0:T(8,128)S(1)}, f32[1,64,512]{2,1,0:T(8,128)S(1)}, u32[]{:S(2)}, u32[]{:S(2)}) collective-permute-start(f32[1,64,512]{2,1,0:T(8,128)S(1)} %get-tuple-element.72), channel_id=1, source_target_pairs={{0,2},{1,3},{2,0},{3,1},{4,6},{5,7},{6,4},{7,5},{8,10},{9,11},{10,... | collective-permute-start | bytes 393224 | tf_op jit(solution)/shard_map/ppermute | solution.py:511
  44.5 55.9 %all-to-all-start = ((f32[32,8,2048]{2,1,0:T(8,128)}), f32[32,8,2048]{2,1,0:T(8,128)}, u32[]{:S(2)}, u32[]{:S(2)}) async-start(f32[32,8,2048]{2,1,0:T(8,128)} %bitcast.6), calls=%async_computation | async-start | bytes 4194304 | tf_op jit(solution)/shard_map/all_to_all | solution.py:515
  62.6 66.9 %collective-permute-start.6 = (f32[3,4096]{1,0:T(4,128)}, f32[3,4096]{1,0:T(4,128)}, u32[]{:S(2)}, u32[]{:S(2)}) collective-permute-start(f32[3,4096]{1,0:T(4,128)} %bitcast.275), channel_id=1, source_target_pairs={{16,0}} | collective-permute-start | bytes 147464 | tf_op jit(solution)/shard_map/ppermute | solution.py:468
  100.4 51.9 %all-to-all-start.1 = ((f32[32,8,1024]{2,1,0:T(8,128)}), f32[32,8,1024]{2,1,0:T(8,128)S(1)}, u32[]{:S(2)}, u32[]{:S(2)}) async-start(f32[32,8,1024]{2,1,0:T(8,128)} %bitcast.11), calls=%async_computation.1 | async-start | bytes 2097152 | tf_op jit(solution)/shard_map/all_to_all | solution.py:515
  152.3 57.3 %all-to-all-start.2 = ((f32[32,8,2048]{2,1,0:T(8,128)}), f32[32,8,2048]{2,1,0:T(8,128)S(1)}, u32[]{:S(2)}, u32[]{:S(2)}) async-start(f32[32,8,2048]{2,1,0:T(8,128)} %bitcast.306), calls=%async_computation.2 | async-start | bytes 4194304 | tf_op jit(solution)/shard_map/all_to_all | solution.py:515
  159.5 19.0 %collective-permute-start.7 = (f32[1,4096]{1,0:T(1,128)}, f32[1,4096]{1,0:T(1,128)}, u32[]{:S(2)}, u32[]{:S(2)}) collective-permute-start(f32[1,4096]{1,0:T(1,128)} %slice_bitcast_fusion.16), channel_id=1, source_target_pairs={{16,0}} | collective-permute-start | bytes 49160 | tf_op jit(solution)/shard_map/ppermute | solution.py:468
  209.6 51.5 %all-to-all-start.3 = ((f32[32,8,1024]{2,1,0:T(8,128)}), f32[32,8,1024]{2,1,0:T(8,128)S(1)}, u32[]{:S(2)}, u32[]{:S(2)}) async-start(f32[32,8,1024]{2,1,0:T(8,128)} %bitcast.281), calls=%async_computation.3 | async-start | bytes 2097152 | tf_op jit(solution)/shard_map/all_to_all | solution.py:515
  232.9 26.1 %collective-permute-start.12 = (f32[2,64,512]{2,1,0:T(8,128)S(1)}, f32[2,64,512]{2,1,0:T(8,128)S(1)}, u32[]{:S(2)}, u32[]{:S(2)}) collective-permute-start(f32[2,64,512]{2,1,0:T(8,128)S(1)} %get-tuple-element.54), channel_id=1, source_target_pairs={{0,2},{1,3},{2,0},{3,1},{4,6},{5,7},{6,4},{7,5},{8,10},{9,11},{10,... | collective-permute-start | bytes 786440 | tf_op jit(solution)/shard_map/ppermute | solution.py:511
  235.3 23.7 %collective-permute-start.13 = (f32[2,64,512]{2,1,0:T(8,128)S(1)}, f32[2,64,512]{2,1,0:T(8,128)S(1)}, u32[]{:S(2)}, u32[]{:S(2)}) collective-permute-start(f32[2,64,512]{2,1,0:T(8,128)S(1)} %get-tuple-element.53), channel_id=1, source_target_pairs={{0,3},{1,2},{2,1},{3,0},{4,7},{5,6},{6,5},{7,4},{8,11},{9,10},{10,... | collective-permute-start | bytes 786440 | tf_op jit(solution)/shard_map/ppermute | solution.py:511
  294.6 21.3 %collective-permute-start.15 = (f32[2,64,512]{2,1,0:T(8,128)S(1)}, f32[2,64,512]{2,1,0:T(8,128)S(1)}, u32[]{:S(2)}, u32[]{:S(2)}) collective-permute-start(f32[2,64,512]{2,1,0:T(8,128)S(1)} %get-tuple-element.51), channel_id=1, source_target_pairs={{0,2},{1,3},{2,0},{3,1},{4,6},{5,7},{6,4},{7,5},{8,10},{9,11},{10,... | collective-permute-start | bytes 786440 | tf_op jit(solution)/shard_map/ppermute | solution.py:511
  295.0 21.0 %collective-permute-start.16 = (f32[2,64,512]{2,1,0:T(8,128)S(1)}, f32[2,64,512]{2,1,0:T(8,128)S(1)}, u32[]{:S(2)}, u32[]{:S(2)}) collective-permute-start(f32[2,64,512]{2,1,0:T(8,128)S(1)} %get-tuple-element.50), channel_id=1, source_target_pairs={{0,3},{1,2},{2,1},{3,0},{4,7},{5,6},{6,5},{7,4},{8,11},{9,10},{10,... | collective-permute-start | bytes 786440 | tf_op jit(solution)/shard_map/ppermute | solution.py:511
  325.1 71.9 %all-to-all-start.4 = ((f32[32,8,2048]{2,1,0:T(8,128)}), f32[32,8,2048]{2,1,0:T(8,128)}, u32[]{:S(2)}, u32[]{:S(2)}) async-start(f32[32,8,2048]{2,1,0:T(8,128)} %bitcast.61), calls=%async_computation.4 | async-start | bytes 4194304 | tf_op jit(solution)/shard_map/all_to_all | solution.py:515
  331.6 37.7 %collective-permute-start.17 = (f32[1,64,512]{2,1,0:T(8,128)S(1)}, f32[1,64,512]{2,1,0:T(8,128)S(1)}, u32[]{:S(2)}, u32[]{:S(2)}) collective-permute-start(f32[1,64,512]{2,1,0:T(8,128)S(1)} %get-tuple-element.66), channel_id=1, source_target_pairs={{0,1},{1,0},{2,3},{3,2},{4,5},{5,4},{6,7},{7,6},{8,9},{9,8},{10,11... | collective-permute-start | bytes 393224 | tf_op jit(solution)/shard_map/ppermute | solution.py:511
  333.4 55.9 %collective-permute-start.18 = (f32[1,64,512]{2,1,0:T(8,128)S(1)}, f32[1,64,512]{2,1,0:T(8,128)S(1)}, u32[]{:S(2)}, u32[]{:S(2)}) collective-permute-start(f32[1,64,512]{2,1,0:T(8,128)S(1)} %get-tuple-element.65), channel_id=1, source_target_pairs={{0,2},{1,3},{2,0},{3,1},{4,6},{5,7},{6,4},{7,5},{8,10},{9,11},{10,... | collective-permute-start | bytes 393224 | tf_op jit(solution)/shard_map/ppermute | solution.py:511
  335.8 53.5 %collective-permute-start.19 = (f32[1,64,512]{2,1,0:T(8,128)S(1)}, f32[1,64,512]{2,1,0:T(8,128)S(1)}, u32[]{:S(2)}, u32[]{:S(2)}) collective-permute-start(f32[1,64,512]{2,1,0:T(8,128)S(1)} %get-tuple-element.64), channel_id=1, source_target_pairs={{0,3},{1,2},{2,1},{3,0},{4,7},{5,6},{6,5},{7,4},{8,11},{9,10},{10,... | collective-permute-start | bytes 393224 | tf_op jit(solution)/shard_map/ppermute | solution.py:511
  397.0 29.7 %all-to-all-start.5 = ((f32[32,8,1024]{2,1,0:T(8,128)}), f32[32,8,1024]{2,1,0:T(8,128)S(1)}, u32[]{:S(2)}, u32[]{:S(2)}) async-start(f32[32,8,1024]{2,1,0:T(8,128)} %bitcast.66), calls=%async_computation.5 | async-start | bytes 2097152 | tf_op jit(solution)/shard_map/all_to_all | solution.py:515
  426.7 51.5 %all-to-all-start.6 = ((f32[32,8,2048]{2,1,0:T(8,128)}), f32[32,8,2048]{2,1,0:T(8,128)S(1)}, u32[]{:S(2)}, u32[]{:S(2)}) async-start(f32[32,8,2048]{2,1,0:T(8,128)} %bitcast.307), calls=%async_computation.6 | async-start | bytes 4194304 | tf_op jit(solution)/shard_map/all_to_all | solution.py:515
  478.2 50.3 %all-to-all-start.7 = ((f32[32,8,1024]{2,1,0:T(8,128)}), f32[32,8,1024]{2,1,0:T(8,128)S(1)}, u32[]{:S(2)}, u32[]{:S(2)}) async-start(f32[32,8,1024]{2,1,0:T(8,128)} %bitcast.282), calls=%async_computation.7 | async-start | bytes 2097152 | tf_op jit(solution)/shard_map/all_to_all | solution.py:515
  495.1 31.3 %collective-permute-start.24 = (f32[2,64,512]{2,1,0:T(8,128)S(1)}, f32[2,64,512]{2,1,0:T(8,128)S(1)}, u32[]{:S(2)}, u32[]{:S(2)}) collective-permute-start(f32[2,64,512]{2,1,0:T(8,128)S(1)} %get-tuple-element.47), channel_id=1, source_target_pairs={{0,2},{1,3},{2,0},{3,1},{4,6},{5,7},{6,4},{7,5},{8,10},{9,11},{10,... | collective-permute-start | bytes 786440 | tf_op jit(solution)/shard_map/ppermute | solution.py:511
  497.5 28.9 %collective-permute-start.25 = (f32[2,64,512]{2,1,0:T(8,128)S(1)}, f32[2,64,512]{2,1,0:T(8,128)S(1)}, u32[]{:S(2)}, u32[]{:S(2)}) collective-permute-start(f32[2,64,512]{2,1,0:T(8,128)S(1)} %get-tuple-element.46), channel_id=1, source_target_pairs={{0,3},{1,2},{2,1},{3,0},{4,7},{5,6},{6,5},{7,4},{8,11},{9,10},{10,... | collective-permute-start | bytes 786440 | tf_op jit(solution)/shard_map/ppermute | solution.py:511
  (93 other events, 598.9 us)

commit v3 on v2

--- a/solution.py
+++ b/solution.py
@@ -114,6 +114,13 @@
         self.steps = self.slots // self.group
         self.freq = n * 2 * self.near
         self.spread = 2 * n * self.near
+        self.split = 4 * n == LANES and self.group == 2
+        lane = np.arange(LANES)
+        self.lane_slot, self.lane_kappa = lane // self.rows, lane % self.rows
+        if self.split:
+            fine = LANES // 4
+            self.lane_slot = lane // fine % 2
+            self.lane_kappa = 2 * (lane % fine) + lane // (2 * fine)
 
     def y_tables(self):
         k1 = np.arange(LANES)
@@ -166,13 +173,12 @@
         angle = 2 * np.pi * np.outer(np.arange(2 * n), np.arange(n)) / (2 * n)
         cos, sin = np.cos(angle), np.sin(angle)
         table = np.stack([np.stack([cos, sin], -1), np.stack([-sin, cos], -1)])
-        full = np.einsum("orsi,fg->orfsig", table, np.eye(self.near))
+        full = np.einsum("orsi,fg->ofrsig", table, np.eye(self.near))
         return full.reshape(2 * self.spread, self.freq)
 
     def x_turn(self):
         angle = -2 * np.pi * np.outer(np.arange(2 * self.devices), np.arange(self.rows))
-        angle = np.repeat(angle / self.len_x, self.near, axis=0)
-        angle = np.tile(angle, (1, self.group))
+        angle = np.tile(angle / self.len_x, (self.near, self.group))
         return np.stack([np.cos(angle), np.sin(angle)]).astype(np.float32)
 
     def x_second(self):
@@ -181,6 +187,7 @@
         cos, sin = np.cos(angle), np.sin(angle)
         table = np.stack([np.stack([cos, -sin], 1), np.stack([sin, cos], 1)])
         full = np.einsum("ixok,qp->iqxopk", table, np.eye(self.group))
+        full = full[:, :, :, :, self.lane_slot, self.lane_kappa]
         return full.reshape(2 * LANES, 2 * LANES)
 
 
@@ -333,9 +340,10 @@
     out_ref[...] = dot_3((back_high[...], back_low[...]), halves(section))
 
 
-def x_stage(plan, data, gains, tables):
+def x_stage(plan, data, gains, group, tables):
     gain, shift, mirror = gains
-    count = (gain.shape[0] + 1) // 2
+    size, index = group
+    count = (size + 1) // 2
     wide = count * LANES
     lane_block = pl.BlockSpec((plan.freq, wide), lambda i: (0, i))
 
@@ -347,9 +355,9 @@
         grid=(plan.steps,),
         in_specs=[
             lane_block,
-            pl.BlockSpec((gain.shape[0], 1, plan.spread, LANES), lambda i: (0, i, 0, 0)),
-            whole(shift),
-            whole(mirror),
+            pl.BlockSpec((size, 1, plan.spread, LANES), lambda i: (index, i, 0, 0)),
+            pl.BlockSpec((size, plan.spread, LANES), lambda i: (index, 0, 0)),
+            pl.BlockSpec((size, plan.spread, LANES), lambda i: (index, 0, 0)),
             *[whole(t) for t in tables],
         ],
         out_specs=lane_block,
@@ -456,54 +464,133 @@
     )(place, data, high, low, turn)
 
 
-def kernel_gains(plan, kernel, diagonal):
+ORDER = (0, 1, 3, 2)
+
+
+def gain_kernel(plan, scale, late_ref, kernel_ref, wave_x_ref, wave_y_ref, out_ref, sort_ref):
+    slots = plan.slots
+    blocks = plan.len_x // LANES
+    row = lax.broadcasted_iota(jnp.int32, (slots, 1), 0)
+    lane = lax.broadcasted_iota(jnp.int32, (1, LANES), 1)
+    swapped = (row == 0) & (late_ref[0] == 1)
+    for block in range(blocks):
+        span = slice(block * LANES, (block + 1) * LANES)
+        value = kernel_ref[0, :slots, span]
+        value = jnp.where(swapped, kernel_ref[0, slots : slots + 1, span], value)
+        sort_ref[pl.ds(block, slots, stride=blocks), :] = value
+    diagonal = jnp.where(pl.program_id(0) == 2, 0.0, scale)
+    half = LANES // 2
+    for pair in range(plan.steps // 2):
+        turned = sort_ref[pair * LANES : (pair + 1) * LANES, :].T
+        low, high = turned[:half], turned[half:]
+        parts = (
+            jnp.where(lane < half, low, pltpu.roll(high, half, 1)),
+            jnp.where(lane < half, pltpu.roll(low, half, 1), high),
+        )
+        for i, part in enumerate(parts):
+            step = 2 * pair + i
+            wave = wave_x_ref[...] + wave_y_ref[0, step : step + 1, :]
+            out_ref[0, step] = diagonal * wave - scale * part
+
+
+def kernel_gains(plan, kernel):
     n, near, slots = plan.devices, plan.near, plan.slots
     me = lax.axis_index(AXES)
     scale = 2.0 / (plan.len_x * plan.len_y)
-    kx = np.arange(plan.len_x)
+    r = np.arange(2 * n)
+    kx = 2 * n * plan.lane_kappa[None] + r[:, None]
     wave_x = jnp.asarray(2 * STIFFNESS * np.cos(2 * np.pi * kx / plan.len_x), jnp.float32)
-    count = kernel.shape[0]
-    diagonal = jnp.asarray(diagonal, jnp.float32)
-
-    nyquist = lax.ppermute(kernel[:, 0, :], AXES, [(n // 2, 0)])
-    split = kernel.reshape(count, near, plan.residues, plan.len_x)
-    first = jnp.where(me < n // 2, split[:, :, :1], split[:, :, slots : slots + 1])
-    chosen = jnp.concatenate([first, split[:, :, 1:slots]], axis=2)
+    late = me >= n // 2
     slot = lax.broadcasted_iota(jnp.int32, (near, slots), 1)
-    slot = jnp.where((slot == 0) & (me >= n // 2), slots, slot)
+    slot = jnp.where((slot == 0) & late, slots, slot)
     ky = (me * near + lax.broadcasted_iota(jnp.int32, (near, slots), 0)) * plan.residues + slot
     wave_y = 2 * STIFFNESS * jnp.cos(ky.astype(jnp.float32) * (2 * math.pi / plan.len_y))
-    wave = wave_x[None, None, :] + wave_y[:, :, None]
-    gain = (diagonal[:, None, None, None] * wave[None] - chosen) * scale
-
-    def arrange(array, count_near, count_slots):
-        group = min(plan.group, count_slots)
-        shaped = array.reshape(count, count_near, count_slots // group, group, plan.rows, 2 * n)
-        moved = shaped.transpose(0, 2, 5, 1, 3, 4)
-        return moved.reshape(count, count_slots // group, 2 * n * count_near, group * plan.rows)
-
-    zero_row = (diagonal[:, None] * (wave_x + 2 * STIFFNESS)[None] - kernel[:, 0, :]) * scale
-    last_row = (diagonal[:, None] * (wave_x - 2 * STIFFNESS)[None] - nyquist) * scale
-    shift = jnp.where(me == 0, 0.25 * (zero_row + last_row) - zero_row, 0.0)
-    mirror = jnp.where(me == 0, 0.25 * (zero_row - last_row), 0.0)
-
-    def place(row):
-        small = row.reshape(count, plan.rows, 2 * n).transpose(0, 2, 1)[:, :, None, :]
-        small = jnp.pad(small, ((0, 0), (0, 0), (0, near - 1), (0, LANES - plan.rows)))
-        return small.reshape(count, plan.spread, LANES)
-
-    arrays = (arrange(gain, near, slots), place(shift), place(mirror))
-    return arrays
+    wave_y = wave_y.reshape(near, plan.steps, plan.group)
+    wave_y = sum(
+        wave_y[:, :, i : i + 1] * jnp.asarray(plan.lane_slot == i, jnp.float32)
+        for i in range(plan.group)
+    )
+    if plan.split:
+        out_shape = (4, plan.steps, plan.spread, LANES)
+        gain = pl.pallas_call(
+            functools.partial(gain_kernel, plan, scale),
+            grid=(4, near),
+            in_specs=[
+                pl.BlockSpec(memory_space=pltpu.SMEM),
+                pl.BlockSpec(
+                    (1, plan.residues, plan.len_x),
+                    lambda c, f: (jnp.where(c < 2, c, 5 - c), f, 0),
+                ),
+                pl.BlockSpec(wave_x.shape, lambda c, f: (0, 0)),
+                pl.BlockSpec((1, plan.steps, LANES), lambda c, f: (f, 0, 0)),
+            ],
+            out_specs=pl.BlockSpec((1, plan.steps, 2 * n, LANES), lambda c, f: (c, 0, f, 0)),
+            out_shape=jax.ShapeDtypeStruct(out_shape, jnp.float32),
+            scratch_shapes=[pltpu.VMEM((slots * plan.len_x // LANES, LANES), jnp.float32)],
+            compiler_params=pltpu.CompilerParams(vmem_limit_bytes=16 * 2**20),
+            cost_estimate=pl.CostEstimate(
+                flops=2**30, bytes_accessed=12 * 2**20, transcendentals=0
+            ),
+            name="gain",
+        )(late.astype(jnp.int32).reshape(1), kernel, wave_x, wave_y)
+    else:
+        kernel_4 = kernel.reshape(4, near, plan.residues, plan.len_x)
+        first = jnp.where(late, kernel_4[:, :, slots : slots + 1], kernel_4[:, :, :1])
+        chosen = jnp.concatenate([first, kernel_4[:, :, 1:slots]], axis=2)
+        shaped = chosen.reshape(4, near, plan.steps, plan.group, plan.rows, 2 * n)
+        moved = shaped.transpose(0, 2, 1, 5, 3, 4).reshape(4, plan.steps, near, 2 * n, LANES)
+        moved = jnp.stack([moved[i] for i in ORDER])
+        wave = wave_x + wave_y.transpose(1, 0, 2)[:, :, None]
+        gain = jnp.concatenate([wave[None] - moved[:2], -moved[2:3], wave[None] - moved[3:]])
+        gain = (scale * gain).reshape(4, plan.steps, plan.spread, LANES)
+
+    nyquist = lax.ppermute(kernel[:, 0, :], AXES, [(n // 2, 0)])
+
+    def arrange(row, wave_y):
+        row = jnp.stack([row[i] for i in ORDER])
+        if plan.split:
+            small = row.reshape(4, plan.rows // 2, 2, 2 * n).transpose(0, 3, 2, 1)
+        else:
+            small = row.reshape(4, plan.rows, 1, 2 * n).transpose(0, 3, 2, 1)
+        small = jnp.pad(small[:, :, :, None], ((0, 0),) * 3 + ((0, plan.group - 1), (0, 0)))
+        small = small.reshape(4, 2 * n, LANES)
+        diagonal = jnp.asarray([1.0, 1.0, 0.0, 1.0], jnp.float32)[:, None, None]
+        return (diagonal * (wave_x + wave_y) - small) * scale
+
+    zero_row = arrange(kernel[:, 0, :], 2 * STIFFNESS)
+    last_row = arrange(nyquist, -2 * STIFFNESS)
+    used = jnp.asarray(plan.lane_slot == 0) & (me == 0)
+
+    def place(rows):
+        rows = jnp.where(used, rows, 0.0)[:, None]
+        rows = jnp.pad(rows, ((0, 0), (0, near - 1), (0, 0), (0, 0)))
+        return rows.reshape(4, plan.spread, LANES)
+
+    shift = place(0.25 * (zero_row + last_row) - zero_row)
+    return gain, shift, place(0.25 * (zero_row - last_row))
 
 
 def cross(left, right):
-    return jnp.stack(
-        [
-            left[1] * right[2] - left[2] * right[1],
-            left[2] * right[0] - left[0] * right[2],
-            left[0] * right[1] - left[1] * right[0],
-        ]
-    )
+    return [
+        left[1] * right[2] - left[2] * right[1],
+        left[2] * right[0] - left[0] * right[2],
+        left[0] * right[1] - left[1] * right[0],
+    ]
+
+
+def inner(left, right):
+    return left[0] * right[0] + left[1] * right[1] + left[2] * right[2]
+
+
+def rate(field, effective):
+    torque = cross(field, effective)
+    again = cross(field, torque)
+    return [-(t + DAMPING * a) / (1.0 + DAMPING * DAMPING) for t, a in zip(torque, again)]
+
+
+def normal(vector, occ):
+    size = jnp.sqrt(inner(vector, vector) + 1.0 - occ)
+    return [v / size for v in vector]
 
 
 def swap(values, axis, offset):
@@ -530,9 +617,7 @@
         *np_halves(plan.x_second()),
         jnp.asarray(plan.x_turn()),
     )
-    gain_b = kernel_gains(plan, kernel_spectrum[2:3], (1.0,))
-    paired = jnp.concatenate([kernel_spectrum[:2], kernel_spectrum[3:]])
-    gain_a = kernel_gains(plan, paired, (1.0, 1.0, 0.0))
+    gains = kernel_gains(plan, kernel_spectrum)
 
     def sent(array):
         return array.reshape(plan.devices, 2 * plan.near, array.shape[1])
@@ -562,40 +647,36 @@
             field = lax.dynamic_update_slice(field, piece, (0, start_row(offset), 0))
         return field
 
-    def effective(field):
-        rows_a = gather_rows(field[:2])
-        rows_b = gather_rows(field[2:])
+    def effective(rows_a, rows_b):
         spectra_a = sent(y_forward(plan, place, rows_a, high, low))
         columns_a = exchange(spectra_a, AXES)
         spectra_b = sent(y_forward(plan, place, rows_b, high, low))
         columns_a, spectra_b = lax.optimization_barrier((columns_a, spectra_b))
         columns_b = exchange(spectra_b, AXES)
-        product_a = sent(x_stage(plan, flat(columns_a), gain_a, tables))
+        product_a = sent(x_stage(plan, flat(columns_a), gains, (1, 3), tables))
         product_a, columns_b = lax.optimization_barrier((product_a, columns_b))
         returned_a = exchange(product_a, AXES)
-        product_b = sent(x_stage(plan, flat(columns_b), gain_b, tables))
+        product_b = sent(x_stage(plan, flat(columns_b), gains, (3, 0), tables))
         returned_a, product_b = lax.optimization_barrier((returned_a, product_b))
         returned_b = exchange(product_b, AXES)
-        spatial_a = y_inverse(plan, place, flat(returned_a), high_back, low_back)
-        field_a = return_rows(spatial_a)
-        spatial_b = y_inverse(plan, place, flat(returned_b), high_back, low_back)
-        field_b = return_rows(spatial_b)
-        return jnp.concatenate([field_a, field_b])
-
-    def rate(field):
-        torque = cross(field, effective(field))
-        return -(torque + DAMPING * cross(field, torque)) / (1.0 + DAMPING * DAMPING)
-
-    def normal(vector):
-        return vector / jnp.sqrt(jnp.sum(vector * vector, axis=0) + 1.0 - occ)[None]
-
-    first = rate(start)
-    middle = normal(start + TIME_STEP * first)
-    second = rate(middle)
-    second = second - jnp.sum(second * start, axis=0)[None] * start
-    mean_rate = 0.5 * (first + second)
-    mag_next = normal(start + TIME_STEP * mean_rate)
-    return (mag_next, mean_rate)
+        field_a = y_inverse(plan, place, flat(returned_a), high_back, low_back)
+        field_b = y_inverse(plan, place, flat(returned_b), high_back, low_back)
+        return [field_b[:, 0], field_b[:, 1], field_a[:, 0]]
+
+    rows_a = gather_rows(start[2:])
+    rows_b = gather_rows(start[:2])
+    field = effective(rows_a, rows_b)
+    begin = [rows_b[:, 0], rows_b[:, 1], rows_a[:, 0]]
+    held = jnp.where(inner(begin, begin) > 0.25, 1.0, 0.0)
+    first = rate(begin, field)
+    middle = normal([b + TIME_STEP * f for b, f in zip(begin, first)], held)
+    field = effective(middle[2][:, None], jnp.stack(middle[:2], axis=1))
+    second = rate(middle, field)
+    along = inner(second, begin)
+    mean = [0.5 * (f + (s - along * b)) for f, s, b in zip(first, second, begin)]
+    mean_rate = return_rows(jnp.stack(mean, axis=1))
+    moved = start + TIME_STEP * mean_rate
+    return (jnp.stack(normal([moved[0], moved[1], moved[2]], occ)), mean_rate)
 
 
 def solution(mesh):

time: 567 us -> 468 us (0.83)
  local copies, waits for them, and re-layouts: 78.2 us -> 33.2 us
  starting transfers between devices: 92.2 us -> 61.5 us
  other arithmetic: 44 us -> 19.4 us
  waiting for transfers between devices: 208 us -> 197 us
  Pallas kernels: 140 us -> 149 us
    ppermute x24 -> x9, waiting for transfers between devices: 162 us -> 72.4 us  [swap(): return lax.ppermute(values, axis, [(i, i ^ offset) for i in range(size)])]
    all_to_all x8, waiting for transfers between devices: 45.9 us -> 125 us  [exchange(): return lax.all_to_all(values, axes, split_axis=0, concat_axis=0, tiled=True)]
    ppermute x24 -> x9, starting transfers between devices: 43.8 us -> 16.3 us  [swap(): return lax.ppermute(values, axis, [(i, i ^ offset) for i in range(size)])]
    transpose x2 -> x0, local copies, waits for them, and re-layouts: 14.4 us -> none  [arrange(): moved = shaped.transpose(0, 2, 5, 1, 3, 4)]
    reshape x8 -> x2, local copies, waits for them, and re-layouts: 13 us -> 0.15 us  [arrange(): small = row.reshape(4, plan.rows // 2, 2, 2 * n).transpose(0, 3, 2, 1)]
    transpose x2 -> x0, other arithmetic: 10.2 us -> none  [arrange(): moved = shaped.transpose(0, 2, 5, 1, 3, 4)]
    concatenate x2 -> x0, local copies, waits for them, and re-layouts: 9.32 us -> none  [kernel_gains(): chosen = jnp.concatenate([first, split[:, :, 1:slots]], axis=2)]
    pallas_call x0 -> x1, Pallas kernels: none -> 6.89 us  [kernel_gains(): pl.pallas_call(functools.partial(gain_kernel, plan, scale), grid=(4, near...]
  transfers between devices with their start and end apart: 34 -> 18, of which waited for: 17 -> 10; matrix products, arithmetic and copies ran while one was open for 15% -> 4% of each run, Pallas kernels for 20% -> 24%
where the time goes in v3:
time: 468 us; the launch traced here: 462 us
  waiting for transfers between devices  197 us (42%)
  Pallas kernels  149 us (32%)
  starting transfers between devices  61.5 us (13%)
  local copies, waits for them, and re-layouts  33.2 us (7%)
  other arithmetic  19.4 us (4%)
    all_to_all x8, waiting for transfers between devices, exchange(): return lax.all_to_all(values, axes, split_axis=0, concat_axis=0, tiled=True)  125 us
    ppermute x9, waiting for transfers between devices, swap(): return lax.ppermute(values, axis, [(i, i ^ offset) for i in range(size)])  72.4 us
    pallas_call x4, Pallas kernels, x_stage(): pl.pallas_call(functools.partial(x_kernel, plan), grid=(plan.steps,), in_...  70.6 us
    all_to_all x8, starting transfers between devices, exchange(): return lax.all_to_all(values, axes, split_axis=0, concat_axis=0, tiled=True)  43.9 us
    pallas_call x4, Pallas kernels, y_inverse(): pl.pallas_call(functools.partial(y_inverse_kernel, plan), grid=(plan.step...  37.7 us
    pallas_call x4, Pallas kernels, y_forward(): pl.pallas_call(functools.partial(y_forward_kernel, plan), grid=(plan.step...  33.4 us
    unnamed x153, local copies, waits for them, and re-layouts  27.7 us
    ppermute x9, starting transfers between devices, swap(): return lax.ppermute(values, axis, [(i, i ^ offset) for i in range(size)])  16.3 us
  transfers between devices with their start and end apart: 18, of which 10 were waited for; matrix products, arithmetic and copies ran while one was open for 4% of the time, Pallas kernels for 24%

profile of v3, /device:TPU:0, one launch (start us, length us, event | category | flops | bytes accessed | tf_op | source)
XLA Modules:
  0.0 462.0 jit_solution(13182054960999767793)
XLA Ops:
  13.2 6.6 %collective-permute-done.4 = f32[1,64,512]{2,1,0:T(8,128)S(1)} collective-permute-done((f32[1,64,512]{2,1,0:T(8,128)S(1)}, f32[1,64,512]{2,1,0:T(8,128)S(1)}, u32[]{:S(2)}, u32[]{:S(2)}) %collective-permute-start.4) | collective-permute-done | bytes 131104 | tf_op jit(solution)/shard_map/ppermute | solution.py:598
  20.5 7.5 %y_forward.4 = f32[256,1024]{1,0:T(8,128)} custom-call(s32[1]{0:T(128)} %bitcast.4.place_ref, f32[4,1,64,512]{3,2,1,0:T(8,128)S(1)} %pad_maximum_fusion.4.rows_ref, bf16[8,256,512]{2,1,0:T(8,128)(2,1)S(1)} %get-tuple-element.53.high_ref, bf16[8,256,512]{2,1,0:T(8,128)(2,1)} %get-tuple-element.52.low_ref), custom_call_target="tpu_custom_call" | custom-call | flops 805306368 | bytes 10485760 | tf_op jit(solution)/shard_map/y_forward/pallas_call | solution.py:246
  38.0 20.2 %collective-permute-done = f32[2,64,512]{2,1,0:T(8,128)S(1)} collective-permute-done((f32[2,64,512]{2,1,0:T(8,128)S(1)}, f32[2,64,512]{2,1,0:T(8,128)S(1)}, u32[]{:S(2)}, u32[]{:S(2)}) %collective-permute-start) | collective-permute-done | bytes 262176 | tf_op jit(solution)/shard_map/ppermute | solution.py:598
  58.2 18.7 %collective-permute-done.1 = f32[2,64,512]{2,1,0:T(8,128)S(1)} collective-permute-done((f32[2,64,512]{2,1,0:T(8,128)S(1)}, f32[2,64,512]{2,1,0:T(8,128)S(1)}, u32[]{:S(2)}, u32[]{:S(2)}) %collective-permute-start.1) | collective-permute-done | bytes 262176 | tf_op jit(solution)/shard_map/ppermute | solution.py:598
  76.9 9.2 %y_forward.5 = f32[256,2048]{1,0:T(8,128)} custom-call(s32[1]{0:T(128)} %bitcast.4.place_ref, f32[4,2,64,512]{3,2,1,0:T(8,128)S(1)} %pad_maximum_fusion.2.rows_ref, bf16[8,256,512]{2,1,0:T(8,128)(2,1)} %copy-done, bf16[8,256,512]{2,1,0:T(8,128)(2,1)} %get-tuple-element.52.low_ref), custom_call_target="tpu_custom_call" | custom-call | flops 1610612736 | bytes 10485760 | tf_op jit(solution)/shard_map/y_forward/pallas_call | solution.py:246
  86.1 7.9 %all-to-all-start.1 = ((f32[32,8,2048]{2,1,0:T(8,128)}), f32[32,8,2048]{2,1,0:T(8,128)}, u32[]{:S(2)}, u32[]{:S(2)}) async-start(f32[32,8,2048]{2,1,0:T(8,128)} %bitcast.10), calls=%async_computation.1 | async-start | bytes 4194304 | tf_op jit(solution)/shard_map/all_to_all | solution.py:602
  101.9 6.9 %gain.1.gain_ref = f32[4,8,256,128]{3,2,1,0:T(8,128)S(1)} custom-call(s32[1]{0:T(128)} %bitcast.12.late_ref, f32[4,128,4096]{2,1,0:T(8,128)S(1)} %copy-done.4, f32[64,128]{1,0:T(8,128)S(1)} %copy-done.19, f32[4,8,128]{2,1,0:T(8,128)S(1)} %multiply_add_fusion.5.wave_y_ref), custom_call_target="tpu_custom_call" | custom-call | flops 1073741824 | bytes 12582912 | tf_op jit(solution)/shard_map/gain/pallas_call | solution.py:515
  117.0 15.1 %x_stage.4 = f32[256,1024]{1,0:T(8,128)} custom-call(f32[256,1024]{1,0:T(8,128)} %bitcast.11.data_ref, f32[4,8,256,128]{3,2,1,0:T(8,128)} %copy-done.7, f32[4,256,128]{2,1,0:T(8,128)S(1)} %bitcast.87, f32[4,256,128]{2,1,0:T(8,128)S(1)} %bitcast.91, bf16[512,256]{1,0:T(8,128)(2,1)S(1)} %copy-done.20, bf16[512,256]{1,0:T(8,128)(2,1)S(1)} %copy-done.21, ...), custom_call_target="tpu_custom_call" | custom-call | flops 3221225472 | bytes 12582912 | tf_op jit(solution)/shard_map/x_stage/pallas_call | solution.py:353
  132.1 8.8 %all-to-all-done.1 = f32[32,8,2048]{2,1,0:T(8,128)} async-done(((f32[32,8,2048]{2,1,0:T(8,128)}), f32[32,8,2048]{2,1,0:T(8,128)}, u32[]{:S(2)}, u32[]{:S(2)}) %all-to-all-start.1) | async-done | bytes 2097184 | tf_op jit(solution)/shard_map/all_to_all | solution.py:602
  150.3 20.2 %x_stage.5 = f32[256,2048]{1,0:T(8,128)} custom-call(f32[256,2048]{1,0:T(8,128)} %bitcast.24.data_ref, f32[4,8,256,128]{3,2,1,0:T(8,128)} %copy-done.7, f32[4,256,128]{2,1,0:T(8,128)S(1)} %bitcast.88, f32[4,256,128]{2,1,0:T(8,128)S(1)} %bitcast.92, bf16[512,256]{1,0:T(8,128)(2,1)S(1)} %copy-done.20, bf16[512,256]{1,0:T(8,128)(2,1)S(1)} %copy-done.22, ...), custom_call_target="tpu_custom_call" | custom-call | flops 6442450944 | bytes 12582912 | tf_op jit(solution)/shard_map/x_stage/pallas_call | solution.py:353
  182.5 8.1 %y_inverse.4 = f32[4,1,64,512]{3,2,1,0:T(8,128)S(1)} custom-call(s32[1]{0:T(128)} %bitcast.4.place_ref, f32[256,1024]{1,0:T(8,128)S(1)} %bitcast.85, bf16[8,512,256]{2,1,0:T(8,128)(2,1)S(1)} %get-tuple-element.51.high_ref, bf16[8,512,256]{2,1,0:T(8,128)(2,1)} %get-tuple-element.50.low_ref, f32[2,16,128]{2,1,0:T(8,128)S(1)} %copy-done.18), custom_call_target="tpu_custom_call" | custom-call | flops 805306368 | bytes 10485760 | tf_op jit(solution)/shard_map/y_inverse/pallas_call | solution.py:441
  191.4 32.9 %all-to-all-done.3 = f32[32,8,2048]{2,1,0:T(8,128)} async-done(((f32[32,8,2048]{2,1,0:T(8,128)}), f32[32,8,2048]{2,1,0:T(8,128)}, u32[]{:S(2)}, u32[]{:S(2)}) %all-to-all-start.3) | async-done | bytes 2097184 | tf_op jit(solution)/shard_map/all_to_all | solution.py:602
  224.3 10.8 %y_inverse.5 = f32[4,2,64,512]{3,2,1,0:T(8,128)S(1)} custom-call(s32[1]{0:T(128)} %bitcast.4.place_ref, f32[256,2048]{1,0:T(8,128)} %bitcast.27.data_ref, bf16[8,512,256]{2,1,0:T(8,128)(2,1)} %copy-done.2, bf16[8,512,256]{2,1,0:T(8,128)(2,1)} %get-tuple-element.50.low_ref, f32[2,16,128]{2,1,0:T(8,128)S(1)} %copy-done.18), custom_call_target="tpu_custom_call" | custom-call | flops 1610612736 | bytes 10485760 | tf_op jit(solution)/shard_map/y_inverse/pallas_call | solution.py:441
  239.2 7.5 %y_forward.6 = f32[256,1024]{1,0:T(8,128)} custom-call(s32[1]{0:T(128)} %bitcast.4.place_ref, f32[4,1,64,512]{3,2,1,0:T(8,128)S(1)} %get-tuple-element.66.rows_ref, bf16[8,256,512]{2,1,0:T(8,128)(2,1)S(1)} %copy-done.1, bf16[8,256,512]{2,1,0:T(8,128)(2,1)} %get-tuple-element.52.low_ref), custom_call_target="tpu_custom_call" | custom-call | flops 805306368 | bytes 10485760 | tf_op jit(solution)/shard_map/y_forward/pallas_call | solution.py:246
  251.4 9.1 %y_forward.7 = f32[256,2048]{1,0:T(8,128)} custom-call(s32[1]{0:T(128)} %bitcast.4.place_ref, f32[4,2,64,512]{3,2,1,0:T(8,128)S(1)} %pad_maximum_fusion.3.rows_ref, bf16[8,256,512]{2,1,0:T(8,128)(2,1)} %copy-done, bf16[8,256,512]{2,1,0:T(8,128)(2,1)} %get-tuple-element.52.low_ref), custom_call_target="tpu_custom_call" | custom-call | flops 1610612736 | bytes 10485760 | tf_op jit(solution)/shard_map/y_forward/pallas_call | solution.py:246
  260.5 15.7 %all-to-all-done.4 = f32[32,8,1024]{2,1,0:T(8,128)S(1)} async-done(((f32[32,8,1024]{2,1,0:T(8,128)}), f32[32,8,1024]{2,1,0:T(8,128)S(1)}, u32[]{:S(2)}, u32[]{:S(2)}) %all-to-all-start.4) | async-done | bytes 1048608 | tf_op jit(solution)/shard_map/all_to_all | solution.py:602
  282.9 15.1 %x_stage.6 = f32[256,1024]{1,0:T(8,128)} custom-call(f32[256,1024]{1,0:T(8,128)} %bitcast.118, f32[4,8,256,128]{3,2,1,0:T(8,128)} %copy-done.7, f32[4,256,128]{2,1,0:T(8,128)S(1)} %bitcast.89, f32[4,256,128]{2,1,0:T(8,128)S(1)} %bitcast.93, bf16[512,256]{1,0:T(8,128)(2,1)S(1)} %copy-done.20, bf16[512,256]{1,0:T(8,128)(2,1)S(1)} %copy-done.23, ...), custom_call_target="tpu_custom_call" | custom-call | flops 3221225472 | bytes 12582912 | tf_op jit(solution)/shard_map/x_stage/pallas_call | solution.py:353
  298.0 30.8 %all-to-all-done.5 = f32[32,8,2048]{2,1,0:T(8,128)} async-done(((f32[32,8,2048]{2,1,0:T(8,128)}), f32[32,8,2048]{2,1,0:T(8,128)}, u32[]{:S(2)}, u32[]{:S(2)}) %all-to-all-start.5) | async-done | bytes 2097184 | tf_op jit(solution)/shard_map/all_to_all | solution.py:602
  338.1 20.2 %x_stage.7 = f32[256,2048]{1,0:T(8,128)} custom-call(f32[256,2048]{1,0:T(8,128)} %bitcast.32.data_ref, f32[4,8,256,128]{3,2,1,0:T(8,128)} %copy-done.7, f32[4,256,128]{2,1,0:T(8,128)S(1)} %bitcast.90, f32[4,256,128]{2,1,0:T(8,128)S(1)} %bitcast.94, bf16[512,256]{1,0:T(8,128)(2,1)S(1)} %copy-done.20, bf16[512,256]{1,0:T(8,128)(2,1)S(1)} %copy-done.24, ...), custom_call_target="tpu_custom_call" | custom-call | flops 6442450944 | bytes 12582912 | tf_op jit(solution)/shard_map/x_stage/pallas_call | solution.py:353
  366.7 7.9 %y_inverse.6 = f32[4,1,64,512]{3,2,1,0:T(8,128)S(1)} custom-call(s32[1]{0:T(128)} %bitcast.4.place_ref, f32[256,1024]{1,0:T(8,128)S(1)} %bitcast.86, bf16[8,512,256]{2,1,0:T(8,128)(2,1)S(1)} %copy-done.3, bf16[8,512,256]{2,1,0:T(8,128)(2,1)} %get-tuple-element.50.low_ref, f32[2,16,128]{2,1,0:T(8,128)S(1)} %copy-done.18), custom_call_target="tpu_custom_call" | custom-call | flops 805306368 | bytes 10485760 | tf_op jit(solution)/shard_map/y_inverse/pallas_call | solution.py:441
  375.4 36.7 %all-to-all-done.7 = f32[32,8,2048]{2,1,0:T(8,128)} async-done(((f32[32,8,2048]{2,1,0:T(8,128)}), f32[32,8,2048]{2,1,0:T(8,128)}, u32[]{:S(2)}, u32[]{:S(2)}) %all-to-all-start.7) | async-done | bytes 2097184 | tf_op jit(solution)/shard_map/all_to_all | solution.py:602
  412.2 10.9 %y_inverse.7 = f32[4,2,64,512]{3,2,1,0:T(8,128)S(1)} custom-call(s32[1]{0:T(128)} %bitcast.4.place_ref, f32[256,2048]{1,0:T(8,128)} %bitcast.35.data_ref, bf16[8,512,256]{2,1,0:T(8,128)(2,1)} %copy-done.2, bf16[8,512,256]{2,1,0:T(8,128)(2,1)} %get-tuple-element.50.low_ref, f32[2,16,128]{2,1,0:T(8,128)S(1)} %copy-done.18), custom_call_target="tpu_custom_call" | custom-call | flops 1610612736 | bytes 10485760 | tf_op jit(solution)/shard_map/y_inverse/pallas_call | solution.py:441
  431.6 13.4 %collective-permute-done.7 = f32[3,64,512]{2,1,0:T(8,128)S(1)} collective-permute-done((f32[3,64,512]{2,1,0:T(8,128)S(1)}, f32[3,64,512]{2,1,0:T(8,128)S(1)}, u32[]{:S(2)}, u32[]{:S(2)}) %collective-permute-start.7) | collective-permute-done | bytes 393248 | tf_op jit(solution)/shard_map/ppermute | solution.py:598
  445.1 13.6 %collective-permute-done.8 = f32[3,64,512]{2,1,0:T(8,128)S(1)} collective-permute-done((f32[3,64,512]{2,1,0:T(8,128)S(1)}, f32[3,64,512]{2,1,0:T(8,128)S(1)}, u32[]{:S(2)}, u32[]{:S(2)}) %collective-permute-start.8) | collective-permute-done | bytes 393248 | tf_op jit(solution)/shard_map/ppermute | solution.py:598
  (237 shorter events, 106.3 us)
Async XLA Ops:
  3.7 16.0 %copy-start.42 = (f32[1,1,64,512]{3,2,1,0:T(8,128)}, f32[1,1,64,512]{3,2,1,0:T(8,128)S(1)}, u32[]{:S(2)}) copy-start(f32[1,1,64,512]{3,2,1,0:T(8,128)S(1)} %get-tuple-element.67) | copy-start | bytes 393220
  3.8 9.4 %collective-permute-start.3 = (f32[1,64,512]{2,1,0:T(8,128)S(1)}, f32[1,64,512]{2,1,0:T(8,128)S(1)}, u32[]{:S(2)}, u32[]{:S(2)}) collective-permute-start(f32[1,64,512]{2,1,0:T(8,128)S(1)} %get-tuple-element.70), channel_id=1, source_target_pairs={{0,1},{1,0},{2,3},{3,2},{4,5},{5,4},{6,7},{7,6},{8,9},{9,8},{10,11... | collective-permute-start | bytes 393224 | tf_op jit(solution)/shard_map/ppermute | solution.py:598
  6.9 12.9 %collective-permute-start.4 = (f32[1,64,512]{2,1,0:T(8,128)S(1)}, f32[1,64,512]{2,1,0:T(8,128)S(1)}, u32[]{:S(2)}, u32[]{:S(2)}) collective-permute-start(f32[1,64,512]{2,1,0:T(8,128)S(1)} %get-tuple-element.69), channel_id=1, source_target_pairs={{0,2},{1,3},{2,0},{3,1},{4,6},{5,7},{6,4},{7,5},{8,10},{9,11},{10,... | collective-permute-start | bytes 393224 | tf_op jit(solution)/shard_map/ppermute | solution.py:598
  9.5 10.3 %collective-permute-start.5 = (f32[1,64,512]{2,1,0:T(8,128)S(1)}, f32[1,64,512]{2,1,0:T(8,128)S(1)}, u32[]{:S(2)}, u32[]{:S(2)}) collective-permute-start(f32[1,64,512]{2,1,0:T(8,128)S(1)} %get-tuple-element.68), channel_id=1, source_target_pairs={{0,3},{1,2},{2,1},{3,0},{4,7},{5,6},{6,5},{7,4},{8,11},{9,10},{10,... | collective-permute-start | bytes 393224 | tf_op jit(solution)/shard_map/ppermute | solution.py:598
  13.2 14.9 %copy-start = (bf16[8,256,512]{2,1,0:T(8,128)(2,1)}, bf16[8,256,512]{2,1,0:T(8,128)(2,1)S(1)}, u32[]{:S(2)}) copy-start(bf16[8,256,512]{2,1,0:T(8,128)(2,1)S(1)} %get-tuple-element.53.high_ref) | copy-start | bytes 6291460
  28.0 58.1 %all-to-all-start = ((f32[32,8,1024]{2,1,0:T(8,128)}), f32[32,8,1024]{2,1,0:T(8,128)}, u32[]{:S(2)}, u32[]{:S(2)}) async-start(f32[32,8,1024]{2,1,0:T(8,128)} %bitcast.9), calls=%async_computation | async-start | bytes 2097152 | tf_op jit(solution)/shard_map/all_to_all | solution.py:602
  33.5 24.6 %collective-permute-start = (f32[2,64,512]{2,1,0:T(8,128)S(1)}, f32[2,64,512]{2,1,0:T(8,128)S(1)}, u32[]{:S(2)}, u32[]{:S(2)}) collective-permute-start(f32[2,64,512]{2,1,0:T(8,128)S(1)} %get-tuple-element.60), channel_id=1, source_target_pairs={{0,1},{1,0},{2,3},{3,2},{4,5},{5,4},{6,7},{7,6},{8,9},{9,8},{10,11... | collective-permute-start | bytes 786440 | tf_op jit(solution)/shard_map/ppermute | solution.py:598
  35.3 41.6 %collective-permute-start.1 = (f32[2,64,512]{2,1,0:T(8,128)S(1)}, f32[2,64,512]{2,1,0:T(8,128)S(1)}, u32[]{:S(2)}, u32[]{:S(2)}) collective-permute-start(f32[2,64,512]{2,1,0:T(8,128)S(1)} %get-tuple-element.59), channel_id=1, source_target_pairs={{0,2},{1,3},{2,0},{3,1},{4,6},{5,7},{6,4},{7,5},{8,10},{9,11},{10,... | collective-permute-start | bytes 786440 | tf_op jit(solution)/shard_map/ppermute | solution.py:598
  37.7 39.1 %collective-permute-start.2 = (f32[2,64,512]{2,1,0:T(8,128)S(1)}, f32[2,64,512]{2,1,0:T(8,128)S(1)}, u32[]{:S(2)}, u32[]{:S(2)}) collective-permute-start(f32[2,64,512]{2,1,0:T(8,128)S(1)} %get-tuple-element.58), channel_id=1, source_target_pairs={{0,3},{1,2},{2,1},{3,0},{4,7},{5,6},{6,5},{7,4},{8,11},{9,10},{10,... | collective-permute-start | bytes 786440 | tf_op jit(solution)/shard_map/ppermute | solution.py:598
  86.1 54.8 %all-to-all-start.1 = ((f32[32,8,2048]{2,1,0:T(8,128)}), f32[32,8,2048]{2,1,0:T(8,128)}, u32[]{:S(2)}, u32[]{:S(2)}) async-start(f32[32,8,2048]{2,1,0:T(8,128)} %bitcast.10), calls=%async_computation.1 | async-start | bytes 4194304 | tf_op jit(solution)/shard_map/all_to_all | solution.py:602
  95.2 15.6 %collective-permute-start.6 = (f32[4,4096]{1,0:T(4,128)S(1)}, f32[4,4096]{1,0:T(4,128)S(1)}, u32[]{:S(2)}, u32[]{:S(2)}) collective-permute-start(f32[4,4096]{1,0:T(4,128)S(1)} %bitcast.125), channel_id=1, source_target_pairs={{16,0}} | collective-permute-start | bytes 196616 | tf_op jit(solution)/shard_map/ppermute | solution.py:547
  114.1 31.4 %copy-start.14 = (f32[4,4,64,128]{3,2,1,0:T(8,128)}, f32[4,4,64,128]{3,2,1,0:T(8,128)S(1)}, u32[]{:S(2)}) copy-start(f32[4,4,64,128]{3,2,1,0:T(8,128)S(1)} %pad.21.clone) | copy-start | bytes 1572868
  115.9 29.6 %copy-start.16 = (f32[4,4,64,128]{3,2,1,0:T(8,128)}, f32[4,4,64,128]{3,2,1,0:T(8,128)S(1)}, u32[]{:S(2)}) copy-start(f32[4,4,64,128]{3,2,1,0:T(8,128)S(1)} %pad.22.clone) | copy-start | bytes 1572868
  141.0 29.5 %all-to-all-start.2 = ((f32[32,8,1024]{2,1,0:T(8,128)}), f32[32,8,1024]{2,1,0:T(8,128)S(1)}, u32[]{:S(2)}, u32[]{:S(2)}) async-start(f32[32,8,1024]{2,1,0:T(8,128)} %bitcast.23), calls=%async_computation.2 | async-start | bytes 2097152 | tf_op jit(solution)/shard_map/all_to_all | solution.py:602
  171.4 52.8 %all-to-all-start.3 = ((f32[32,8,2048]{2,1,0:T(8,128)}), f32[32,8,2048]{2,1,0:T(8,128)}, u32[]{:S(2)}, u32[]{:S(2)}) async-start(f32[32,8,2048]{2,1,0:T(8,128)} %bitcast.116), calls=%async_computation.3 | async-start | bytes 4194304 | tf_op jit(solution)/shard_map/all_to_all | solution.py:602
  246.7 29.5 %all-to-all-start.4 = ((f32[32,8,1024]{2,1,0:T(8,128)}), f32[32,8,1024]{2,1,0:T(8,128)S(1)}, u32[]{:S(2)}, u32[]{:S(2)}) async-start(f32[32,8,1024]{2,1,0:T(8,128)} %bitcast.28), calls=%async_computation.4 | async-start | bytes 2097152 | tf_op jit(solution)/shard_map/all_to_all | solution.py:602
  277.2 51.6 %all-to-all-start.5 = ((f32[32,8,2048]{2,1,0:T(8,128)}), f32[32,8,2048]{2,1,0:T(8,128)}, u32[]{:S(2)}, u32[]{:S(2)}) async-start(f32[32,8,2048]{2,1,0:T(8,128)} %bitcast.29), calls=%async_computation.5 | async-start | bytes 4194304 | tf_op jit(solution)/shard_map/all_to_all | solution.py:602
  328.8 29.5 %all-to-all-start.6 = ((f32[32,8,1024]{2,1,0:T(8,128)}), f32[32,8,1024]{2,1,0:T(8,128)S(1)}, u32[]{:S(2)}, u32[]{:S(2)}) async-start(f32[32,8,1024]{2,1,0:T(8,128)} %bitcast.31), calls=%async_computation.6 | async-start | bytes 2097152 | tf_op jit(solution)/shard_map/all_to_all | solution.py:602
  359.3 52.8 %all-to-all-start.7 = ((f32[32,8,2048]{2,1,0:T(8,128)}), f32[32,8,2048]{2,1,0:T(8,128)}, u32[]{:S(2)}, u32[]{:S(2)}) async-start(f32[32,8,2048]{2,1,0:T(8,128)} %bitcast.117), calls=%async_computation.7 | async-start | bytes 4194304 | tf_op jit(solution)/shard_map/all_to_all | solution.py:602
  425.3 19.7 %collective-permute-start.7 = (f32[3,64,512]{2,1,0:T(8,128)S(1)}, f32[3,64,512]{2,1,0:T(8,128)S(1)}, u32[]{:S(2)}, u32[]{:S(2)}) collective-permute-start(f32[3,64,512]{2,1,0:T(8,128)S(1)} %get-tuple-element.56), channel_id=1, source_target_pairs={{0,1},{1,0},{2,3},{3,2},{4,5},{5,4},{6,7},{7,6},{8,9},{9,8},{10,11... | collective-permute-start | bytes 1179656 | tf_op jit(solution)/shard_map/ppermute | solution.py:598
  428.9 29.7 %collective-permute-start.8 = (f32[3,64,512]{2,1,0:T(8,128)S(1)}, f32[3,64,512]{2,1,0:T(8,128)S(1)}, u32[]{:S(2)}, u32[]{:S(2)}) collective-permute-start(f32[3,64,512]{2,1,0:T(8,128)S(1)} %get-tuple-element.55), channel_id=1, source_target_pairs={{0,2},{1,3},{2,0},{3,1},{4,6},{5,7},{6,4},{7,5},{8,10},{9,11},{10,... | collective-permute-start | bytes 1179656 | tf_op jit(solution)/shard_map/ppermute | solution.py:598
  429.2 29.5 %collective-permute-start.9 = (f32[3,64,512]{2,1,0:T(8,128)S(1)}, f32[3,64,512]{2,1,0:T(8,128)S(1)}, u32[]{:S(2)}, u32[]{:S(2)}) collective-permute-start(f32[3,64,512]{2,1,0:T(8,128)S(1)} %get-tuple-element.54), channel_id=1, source_target_pairs={{0,3},{1,2},{2,1},{3,0},{4,7},{5,6},{6,5},{7,4},{8,11},{9,10},{10,... | collective-permute-start | bytes 1179656 | tf_op jit(solution)/shard_map/ppermute | solution.py:598
  431.6 27.2 %copy-start.58 = (f32[3,256,512]{2,1,0:T(8,128)S(1)}, f32[3,256,512]{2,1,0:T(8,128)}, u32[]{:S(2)}) copy-start(f32[3,256,512]{2,1,0:T(8,128)} %param.25) | copy-start | bytes 4718596
  431.6 27.2 %copy-start.63 = (f32[256,512]{1,0:T(8,128)S(1)}, f32[256,512]{1,0:T(8,128)}, u32[]{:S(2)}) copy-start(f32[256,512]{1,0:T(8,128)} %copy-done.62) | copy-start | bytes 1572868
  (69 other events, 346.0 us)

commit v4 on v3

--- a/solution.py
+++ b/solution.py
@@ -113,6 +113,7 @@
         self.group = LANES // self.rows
         self.steps = self.slots // self.group
         self.freq = n * 2 * self.near
+        self.pair = math.gcd(4, self.steps)
         self.spread = 2 * n * self.near
         self.split = 4 * n == LANES and self.group == 2
         lane = np.arange(LANES)
@@ -235,24 +236,29 @@
 
         lax.fori_loop(0, rows_ref.shape[1] * per, one, 0)
 
-    left = (high_ref[0], low_ref[0])
-    out_ref[...] = dot_3(left, (z_high[step], z_low[step]), NT)
+    wide = z_high.shape[1]
+    for part in range(plan.pair):
+        place = step * plan.pair + part
+        left = (high_ref[part], low_ref[part])
+        out_ref[:, part * wide : (part + 1) * wide] = dot_3(
+            left, (z_high[place], z_low[place]), NT
+        )
 
 
 def y_forward(plan, place, rows, high, low):
     wide = rows.shape[1] * LANES
     deep = plan.group * 2 * LANES
-    matrix = pl.BlockSpec((1, plan.freq, deep), lambda i: (i, 0, 0))
+    matrix = pl.BlockSpec((plan.pair, plan.freq, deep), lambda i: (i, 0, 0))
     return pl.pallas_call(
         functools.partial(y_forward_kernel, plan),
-        grid=(plan.steps,),
+        grid=(plan.steps // plan.pair,),
         in_specs=[
             pl.BlockSpec(memory_space=pltpu.SMEM),
             pl.BlockSpec(rows.shape, lambda i: (0, 0, 0, 0)),
             matrix,
             matrix,
         ],
-        out_specs=pl.BlockSpec((plan.freq, wide), lambda i: (0, i)),
+        out_specs=pl.BlockSpec((plan.freq, plan.pair * wide), lambda i: (0, i)),
         out_shape=jax.ShapeDtypeStruct((plan.freq, wide * plan.steps), jnp.float32),
         scratch_shapes=[
             pltpu.VMEM((plan.steps, wide, deep), jnp.bfloat16),
@@ -375,23 +381,24 @@
 
 def y_inverse_kernel(plan, place_ref, data_ref, high_ref, low_ref, turn_ref, out_ref, inner_ref, sum_ref):
     step = pl.program_id(0)
-    value = dot_3((high_ref[0], low_ref[0]), halves(data_ref[...]))
     deep = 2 * LANES
     lane = lax.broadcasted_iota(jnp.int32, (1, LANES), 1)
     count = out_ref.shape[1]
-    for comp in range(count):
-        mixed = value[:deep, comp * LANES : (comp + 1) * LANES]
-        for inner in range(1, plan.group):
-            mixed = jnp.where(
-                lane // plan.rows == inner,
-                value[inner * deep : (inner + 1) * deep, comp * LANES : (comp + 1) * LANES],
-                mixed,
-            )
-        inner_ref[comp, step] = mixed
-
-    @pl.when(step == plan.steps - 1)
+    wide = count * LANES
+    for part in range(plan.pair):
+        data = halves(data_ref[:, part * wide : (part + 1) * wide])
+        value = dot_3((high_ref[part], low_ref[part]), data)
+        for comp in range(count):
+            span = slice(comp * LANES, (comp + 1) * LANES)
+            mixed = value[:deep, span]
+            for inner in range(1, plan.group):
+                other = value[inner * deep : (inner + 1) * deep, span]
+                mixed = jnp.where(lane // plan.rows == inner, other, mixed)
+            inner_ref[comp, step * plan.pair + part] = mixed
+
+    @pl.when(step == plan.steps // plan.pair - 1)
     def _():
-        chunk = 8
+        chunk = 16
         blocks = plan.block_y // LANES
 
         def one_comp(comp, carry):
@@ -433,17 +440,17 @@
     wide = data.shape[1] // plan.steps
     count = wide // LANES
     deep = plan.group * 2 * LANES
-    matrix = pl.BlockSpec((1, deep, plan.freq), lambda i: (i, 0, 0))
+    matrix = pl.BlockSpec((plan.pair, deep, plan.freq), lambda i: (i, 0, 0))
     shape = (plan.n_ty, count, plan.rows, plan.block_y)
     inner = np.arange(LANES) // plan.rows
     angle = 2 * np.pi * np.outer(np.arange(plan.slots), inner) / plan.residues
     turn = jnp.asarray(np.stack([np.cos(angle), np.sin(angle)]), jnp.float32)
     return pl.pallas_call(
         functools.partial(y_inverse_kernel, plan),
-        grid=(plan.steps,),
+        grid=(plan.steps // plan.pair,),
         in_specs=[
             pl.BlockSpec(memory_space=pltpu.SMEM),
-            pl.BlockSpec((plan.freq, wide), lambda i: (0, i)),
+            pl.BlockSpec((plan.freq, plan.pair * wide), lambda i: (0, i)),
             matrix,
             matrix,
             pl.BlockSpec(turn.shape, lambda i: (0, 0, 0)),

time: 468 us -> 451 us (0.964)
  Pallas kernels: 149 us -> 123 us
  waiting for transfers between devices: 197 us -> 206 us
    pallas_call x4, Pallas kernels: 37.7 us -> 24.1 us  [y_inverse(): pl.pallas_call(functools.partial(y_inverse_kernel, plan), grid=(plan.step...]
    pallas_call x4, Pallas kernels: 33.4 us -> 21.9 us  [y_forward(): pl.pallas_call(functools.partial(y_forward_kernel, plan), grid=(plan.step...]
    all_to_all x8, waiting for transfers between devices: 125 us -> 134 us  [exchange(): return lax.all_to_all(values, axes, split_axis=0, concat_axis=0, tiled=True)]
  transfers between devices with their start and end apart: 18 -> 18, of which waited for: 10 -> 10; matrix products, arithmetic and copies ran while one was open for 4% -> 4% of each run, Pallas kernels for 24% -> 22%
where the time goes in v4:
time: 451 us; the launch traced here: 446 us
  waiting for transfers between devices  206 us (46%)
  Pallas kernels  123 us (27%)
  starting transfers between devices  61.5 us (14%)
  local copies, waits for them, and re-layouts  33.2 us (7%)
  other arithmetic  19.4 us (4%)
    all_to_all x8, waiting for transfers between devices, exchange(): return lax.all_to_all(values, axes, split_axis=0, concat_axis=0, tiled=True)  134 us
    ppermute x9, waiting for transfers between devices, swap(): return lax.ppermute(values, axis, [(i, i ^ offset) for i in range(size)])  72.4 us
    pallas_call x4, Pallas kernels, x_stage(): pl.pallas_call(functools.partial(x_kernel, plan), grid=(plan.steps,), in_...  70.6 us
    all_to_all x8, starting transfers between devices, exchange(): return lax.all_to_all(values, axes, split_axis=0, concat_axis=0, tiled=True)  43.9 us
    unnamed x153, local copies, waits for them, and re-layouts  27.7 us
    pallas_call x4, Pallas kernels, y_inverse(): pl.pallas_call(functools.partial(y_inverse_kernel, plan), grid=(plan.step...  24.1 us
    pallas_call x4, Pallas kernels, y_forward(): pl.pallas_call(functools.partial(y_forward_kernel, plan), grid=(plan.step...  21.9 us
    ppermute x9, starting transfers between devices, swap(): return lax.ppermute(values, axis, [(i, i ^ offset) for i in range(size)])  16.3 us
  transfers between devices with their start and end apart: 18, of which 10 were waited for; matrix products, arithmetic and copies ran while one was open for 4% of the time, Pallas kernels for 22%

profile of v4, /device:TPU:0, one launch (start us, length us, event | category | flops | bytes accessed | tf_op | source)
XLA Modules:
  0.0 445.7 jit_solution(6842554265073277931)
XLA Ops:
  13.2 6.6 %collective-permute-done.4 = f32[1,64,512]{2,1,0:T(8,128)S(1)} collective-permute-done((f32[1,64,512]{2,1,0:T(8,128)S(1)}, f32[1,64,512]{2,1,0:T(8,128)S(1)}, u32[]{:S(2)}, u32[]{:S(2)}) %collective-permute-start.4) | collective-permute-done | bytes 131104 | tf_op jit(solution)/shard_map/ppermute | solution.py:605
  25.3 5.3 %all-to-all-start = ((f32[32,8,1024]{2,1,0:T(8,128)}), f32[32,8,1024]{2,1,0:T(8,128)}, u32[]{:S(2)}, u32[]{:S(2)}) async-start(f32[32,8,1024]{2,1,0:T(8,128)} %bitcast.9), calls=%async_computation | async-start | bytes 2097152 | tf_op jit(solution)/shard_map/all_to_all | solution.py:609
  35.2 20.2 %collective-permute-done = f32[2,64,512]{2,1,0:T(8,128)S(1)} collective-permute-done((f32[2,64,512]{2,1,0:T(8,128)S(1)}, f32[2,64,512]{2,1,0:T(8,128)S(1)}, u32[]{:S(2)}, u32[]{:S(2)}) %collective-permute-start) | collective-permute-done | bytes 262176 | tf_op jit(solution)/shard_map/ppermute | solution.py:605
  55.4 18.7 %collective-permute-done.1 = f32[2,64,512]{2,1,0:T(8,128)S(1)} collective-permute-done((f32[2,64,512]{2,1,0:T(8,128)S(1)}, f32[2,64,512]{2,1,0:T(8,128)S(1)}, u32[]{:S(2)}, u32[]{:S(2)}) %collective-permute-start.1) | collective-permute-done | bytes 262176 | tf_op jit(solution)/shard_map/ppermute | solution.py:605
  74.2 6.2 %y_forward.5 = f32[256,2048]{1,0:T(8,128)} custom-call(s32[1]{0:T(128)} %bitcast.4.place_ref, f32[4,2,64,512]{3,2,1,0:T(8,128)S(1)} %pad_maximum_fusion.2.rows_ref, bf16[8,256,512]{2,1,0:T(8,128)(2,1)} %copy-done, bf16[8,256,512]{2,1,0:T(8,128)(2,1)} %get-tuple-element.52.low_ref), custom_call_target="tpu_custom_call" | custom-call | flops 1610612736 | bytes 10485760 | tf_op jit(solution)/shard_map/y_forward/pallas_call | solution.py:252
  80.4 7.9 %all-to-all-start.1 = ((f32[32,8,2048]{2,1,0:T(8,128)}), f32[32,8,2048]{2,1,0:T(8,128)}, u32[]{:S(2)}, u32[]{:S(2)}) async-start(f32[32,8,2048]{2,1,0:T(8,128)} %bitcast.10), calls=%async_computation.1 | async-start | bytes 4194304 | tf_op jit(solution)/shard_map/all_to_all | solution.py:609
  96.2 6.9 %gain.1.gain_ref = f32[4,8,256,128]{3,2,1,0:T(8,128)S(1)} custom-call(s32[1]{0:T(128)} %bitcast.12.late_ref, f32[4,128,4096]{2,1,0:T(8,128)S(1)} %copy-done.4, f32[64,128]{1,0:T(8,128)S(1)} %copy-done.19, f32[4,8,128]{2,1,0:T(8,128)S(1)} %multiply_add_fusion.5.wave_y_ref), custom_call_target="tpu_custom_call" | custom-call | flops 1073741824 | bytes 12582912 | tf_op jit(solution)/shard_map/gain/pallas_call | solution.py:522
  111.3 15.1 %x_stage.4 = f32[256,1024]{1,0:T(8,128)} custom-call(f32[256,1024]{1,0:T(8,128)} %bitcast.11.data_ref, f32[4,8,256,128]{3,2,1,0:T(8,128)} %copy-done.7, f32[4,256,128]{2,1,0:T(8,128)S(1)} %bitcast.87, f32[4,256,128]{2,1,0:T(8,128)S(1)} %bitcast.91, bf16[512,256]{1,0:T(8,128)(2,1)S(1)} %copy-done.20, bf16[512,256]{1,0:T(8,128)(2,1)S(1)} %copy-done.21, ...), custom_call_target="tpu_custom_call" | custom-call | flops 3221225472 | bytes 12582912 | tf_op jit(solution)/shard_map/x_stage/pallas_call | solution.py:359
  126.4 8.8 %all-to-all-done.1 = f32[32,8,2048]{2,1,0:T(8,128)} async-done(((f32[32,8,2048]{2,1,0:T(8,128)}), f32[32,8,2048]{2,1,0:T(8,128)}, u32[]{:S(2)}, u32[]{:S(2)}) %all-to-all-start.1) | async-done | bytes 2097184 | tf_op jit(solution)/shard_map/all_to_all | solution.py:609
  144.5 20.2 %x_stage.5 = f32[256,2048]{1,0:T(8,128)} custom-call(f32[256,2048]{1,0:T(8,128)} %bitcast.24.data_ref, f32[4,8,256,128]{3,2,1,0:T(8,128)} %copy-done.7, f32[4,256,128]{2,1,0:T(8,128)S(1)} %bitcast.88, f32[4,256,128]{2,1,0:T(8,128)S(1)} %bitcast.92, bf16[512,256]{1,0:T(8,128)(2,1)S(1)} %copy-done.20, bf16[512,256]{1,0:T(8,128)(2,1)S(1)} %copy-done.22, ...), custom_call_target="tpu_custom_call" | custom-call | flops 6442450944 | bytes 12582912 | tf_op jit(solution)/shard_map/x_stage/pallas_call | solution.py:359
  165.7 6.1 %all-to-all-start.3 = ((f32[32,8,2048]{2,1,0:T(8,128)}), f32[32,8,2048]{2,1,0:T(8,128)}, u32[]{:S(2)}, u32[]{:S(2)}) async-start(f32[32,8,2048]{2,1,0:T(8,128)} %bitcast.116), calls=%async_computation.3 | async-start | bytes 4194304 | tf_op jit(solution)/shard_map/all_to_all | solution.py:609
  176.7 5.4 %y_inverse.4 = f32[4,1,64,512]{3,2,1,0:T(8,128)S(1)} custom-call(s32[1]{0:T(128)} %bitcast.4.place_ref, f32[256,1024]{1,0:T(8,128)S(1)} %bitcast.85, bf16[8,512,256]{2,1,0:T(8,128)(2,1)S(1)} %get-tuple-element.51.high_ref, bf16[8,512,256]{2,1,0:T(8,128)(2,1)} %get-tuple-element.50.low_ref, f32[2,16,128]{2,1,0:T(8,128)S(1)} %copy-done.18), custom_call_target="tpu_custom_call" | custom-call | flops 805306368 | bytes 10485760 | tf_op jit(solution)/shard_map/y_inverse/pallas_call | solution.py:448
  183.0 35.6 %all-to-all-done.3 = f32[32,8,2048]{2,1,0:T(8,128)} async-done(((f32[32,8,2048]{2,1,0:T(8,128)}), f32[32,8,2048]{2,1,0:T(8,128)}, u32[]{:S(2)}, u32[]{:S(2)}) %all-to-all-start.3) | async-done | bytes 2097184 | tf_op jit(solution)/shard_map/all_to_all | solution.py:609
  218.5 6.9 %y_inverse.5 = f32[4,2,64,512]{3,2,1,0:T(8,128)S(1)} custom-call(s32[1]{0:T(128)} %bitcast.4.place_ref, f32[256,2048]{1,0:T(8,128)} %bitcast.27.data_ref, bf16[8,512,256]{2,1,0:T(8,128)(2,1)} %copy-done.2, bf16[8,512,256]{2,1,0:T(8,128)(2,1)} %get-tuple-element.50.low_ref, f32[2,16,128]{2,1,0:T(8,128)S(1)} %copy-done.18), custom_call_target="tpu_custom_call" | custom-call | flops 1610612736 | bytes 10485760 | tf_op jit(solution)/shard_map/y_inverse/pallas_call | solution.py:448
  239.0 6.2 %y_forward.7 = f32[256,2048]{1,0:T(8,128)} custom-call(s32[1]{0:T(128)} %bitcast.4.place_ref, f32[4,2,64,512]{3,2,1,0:T(8,128)S(1)} %pad_maximum_fusion.3.rows_ref, bf16[8,256,512]{2,1,0:T(8,128)(2,1)} %copy-done, bf16[8,256,512]{2,1,0:T(8,128)(2,1)} %get-tuple-element.52.low_ref), custom_call_target="tpu_custom_call" | custom-call | flops 1610612736 | bytes 10485760 | tf_op jit(solution)/shard_map/y_forward/pallas_call | solution.py:252
  245.2 18.6 %all-to-all-done.4 = f32[32,8,1024]{2,1,0:T(8,128)S(1)} async-done(((f32[32,8,1024]{2,1,0:T(8,128)}), f32[32,8,1024]{2,1,0:T(8,128)S(1)}, u32[]{:S(2)}, u32[]{:S(2)}) %all-to-all-start.4) | async-done | bytes 1048608 | tf_op jit(solution)/shard_map/all_to_all | solution.py:609
  270.5 15.1 %x_stage.6 = f32[256,1024]{1,0:T(8,128)} custom-call(f32[256,1024]{1,0:T(8,128)} %bitcast.118, f32[4,8,256,128]{3,2,1,0:T(8,128)} %copy-done.7, f32[4,256,128]{2,1,0:T(8,128)S(1)} %bitcast.89, f32[4,256,128]{2,1,0:T(8,128)S(1)} %bitcast.93, bf16[512,256]{1,0:T(8,128)(2,1)S(1)} %copy-done.20, bf16[512,256]{1,0:T(8,128)(2,1)S(1)} %copy-done.23, ...), custom_call_target="tpu_custom_call" | custom-call | flops 3221225472 | bytes 12582912 | tf_op jit(solution)/shard_map/x_stage/pallas_call | solution.py:359
  285.6 30.8 %all-to-all-done.5 = f32[32,8,2048]{2,1,0:T(8,128)} async-done(((f32[32,8,2048]{2,1,0:T(8,128)}), f32[32,8,2048]{2,1,0:T(8,128)}, u32[]{:S(2)}, u32[]{:S(2)}) %all-to-all-start.5) | async-done | bytes 2097184 | tf_op jit(solution)/shard_map/all_to_all | solution.py:609
  325.7 20.2 %x_stage.7 = f32[256,2048]{1,0:T(8,128)} custom-call(f32[256,2048]{1,0:T(8,128)} %bitcast.32.data_ref, f32[4,8,256,128]{3,2,1,0:T(8,128)} %copy-done.7, f32[4,256,128]{2,1,0:T(8,128)S(1)} %bitcast.90, f32[4,256,128]{2,1,0:T(8,128)S(1)} %bitcast.94, bf16[512,256]{1,0:T(8,128)(2,1)S(1)} %copy-done.20, bf16[512,256]{1,0:T(8,128)(2,1)S(1)} %copy-done.24, ...), custom_call_target="tpu_custom_call" | custom-call | flops 6442450944 | bytes 12582912 | tf_op jit(solution)/shard_map/x_stage/pallas_call | solution.py:359
  346.9 6.2 %all-to-all-start.7 = ((f32[32,8,2048]{2,1,0:T(8,128)}), f32[32,8,2048]{2,1,0:T(8,128)}, u32[]{:S(2)}, u32[]{:S(2)}) async-start(f32[32,8,2048]{2,1,0:T(8,128)} %bitcast.117), calls=%async_computation.7 | async-start | bytes 4194304 | tf_op jit(solution)/shard_map/all_to_all | solution.py:609
  359.8 39.9 %all-to-all-done.7 = f32[32,8,2048]{2,1,0:T(8,128)} async-done(((f32[32,8,2048]{2,1,0:T(8,128)}), f32[32,8,2048]{2,1,0:T(8,128)}, u32[]{:S(2)}, u32[]{:S(2)}) %all-to-all-start.7) | async-done | bytes 2097184 | tf_op jit(solution)/shard_map/all_to_all | solution.py:609
  399.8 7.0 %y_inverse.7 = f32[4,2,64,512]{3,2,1,0:T(8,128)S(1)} custom-call(s32[1]{0:T(128)} %bitcast.4.place_ref, f32[256,2048]{1,0:T(8,128)} %bitcast.35.data_ref, bf16[8,512,256]{2,1,0:T(8,128)(2,1)} %copy-done.2, bf16[8,512,256]{2,1,0:T(8,128)(2,1)} %get-tuple-element.50.low_ref, f32[2,16,128]{2,1,0:T(8,128)S(1)} %copy-done.18), custom_call_target="tpu_custom_call" | custom-call | flops 1610612736 | bytes 10485760 | tf_op jit(solution)/shard_map/y_inverse/pallas_call | solution.py:448
  415.4 13.4 %collective-permute-done.7 = f32[3,64,512]{2,1,0:T(8,128)S(1)} collective-permute-done((f32[3,64,512]{2,1,0:T(8,128)S(1)}, f32[3,64,512]{2,1,0:T(8,128)S(1)}, u32[]{:S(2)}, u32[]{:S(2)}) %collective-permute-start.7) | collective-permute-done | bytes 393248 | tf_op jit(solution)/shard_map/ppermute | solution.py:605
  428.8 13.6 %collective-permute-done.8 = f32[3,64,512]{2,1,0:T(8,128)S(1)} collective-permute-done((f32[3,64,512]{2,1,0:T(8,128)S(1)}, f32[3,64,512]{2,1,0:T(8,128)S(1)}, u32[]{:S(2)}, u32[]{:S(2)}) %collective-permute-start.8) | collective-permute-done | bytes 393248 | tf_op jit(solution)/shard_map/ppermute | solution.py:605
  (237 shorter events, 102.9 us)
Async XLA Ops:
  3.7 16.0 %copy-start.42 = (f32[1,1,64,512]{3,2,1,0:T(8,128)}, f32[1,1,64,512]{3,2,1,0:T(8,128)S(1)}, u32[]{:S(2)}) copy-start(f32[1,1,64,512]{3,2,1,0:T(8,128)S(1)} %get-tuple-element.67) | copy-start | bytes 393220
  3.8 9.4 %collective-permute-start.3 = (f32[1,64,512]{2,1,0:T(8,128)S(1)}, f32[1,64,512]{2,1,0:T(8,128)S(1)}, u32[]{:S(2)}, u32[]{:S(2)}) collective-permute-start(f32[1,64,512]{2,1,0:T(8,128)S(1)} %get-tuple-element.70), channel_id=1, source_target_pairs={{0,1},{1,0},{2,3},{3,2},{4,5},{5,4},{6,7},{7,6},{8,9},{9,8},{10,11... | collective-permute-start | bytes 393224 | tf_op jit(solution)/shard_map/ppermute | solution.py:605
  6.9 12.9 %collective-permute-start.4 = (f32[1,64,512]{2,1,0:T(8,128)S(1)}, f32[1,64,512]{2,1,0:T(8,128)S(1)}, u32[]{:S(2)}, u32[]{:S(2)}) collective-permute-start(f32[1,64,512]{2,1,0:T(8,128)S(1)} %get-tuple-element.69), channel_id=1, source_target_pairs={{0,2},{1,3},{2,0},{3,1},{4,6},{5,7},{6,4},{7,5},{8,10},{9,11},{10,... | collective-permute-start | bytes 393224 | tf_op jit(solution)/shard_map/ppermute | solution.py:605
  9.5 10.3 %collective-permute-start.5 = (f32[1,64,512]{2,1,0:T(8,128)S(1)}, f32[1,64,512]{2,1,0:T(8,128)S(1)}, u32[]{:S(2)}, u32[]{:S(2)}) collective-permute-start(f32[1,64,512]{2,1,0:T(8,128)S(1)} %get-tuple-element.68), channel_id=1, source_target_pairs={{0,3},{1,2},{2,1},{3,0},{4,7},{5,6},{6,5},{7,4},{8,11},{9,10},{10,... | collective-permute-start | bytes 393224 | tf_op jit(solution)/shard_map/ppermute | solution.py:605
  25.3 55.1 %all-to-all-start = ((f32[32,8,1024]{2,1,0:T(8,128)}), f32[32,8,1024]{2,1,0:T(8,128)}, u32[]{:S(2)}, u32[]{:S(2)}) async-start(f32[32,8,1024]{2,1,0:T(8,128)} %bitcast.9), calls=%async_computation | async-start | bytes 2097152 | tf_op jit(solution)/shard_map/all_to_all | solution.py:609
  30.8 24.6 %collective-permute-start = (f32[2,64,512]{2,1,0:T(8,128)S(1)}, f32[2,64,512]{2,1,0:T(8,128)S(1)}, u32[]{:S(2)}, u32[]{:S(2)}) collective-permute-start(f32[2,64,512]{2,1,0:T(8,128)S(1)} %get-tuple-element.60), channel_id=1, source_target_pairs={{0,1},{1,0},{2,3},{3,2},{4,5},{5,4},{6,7},{7,6},{8,9},{9,8},{10,11... | collective-permute-start | bytes 786440 | tf_op jit(solution)/shard_map/ppermute | solution.py:605
  32.5 41.6 %collective-permute-start.1 = (f32[2,64,512]{2,1,0:T(8,128)S(1)}, f32[2,64,512]{2,1,0:T(8,128)S(1)}, u32[]{:S(2)}, u32[]{:S(2)}) collective-permute-start(f32[2,64,512]{2,1,0:T(8,128)S(1)} %get-tuple-element.59), channel_id=1, source_target_pairs={{0,2},{1,3},{2,0},{3,1},{4,6},{5,7},{6,4},{7,5},{8,10},{9,11},{10,... | collective-permute-start | bytes 786440 | tf_op jit(solution)/shard_map/ppermute | solution.py:605
  35.0 39.1 %collective-permute-start.2 = (f32[2,64,512]{2,1,0:T(8,128)S(1)}, f32[2,64,512]{2,1,0:T(8,128)S(1)}, u32[]{:S(2)}, u32[]{:S(2)}) collective-permute-start(f32[2,64,512]{2,1,0:T(8,128)S(1)} %get-tuple-element.58), channel_id=1, source_target_pairs={{0,3},{1,2},{2,1},{3,0},{4,7},{5,6},{6,5},{7,4},{8,11},{9,10},{10,... | collective-permute-start | bytes 786440 | tf_op jit(solution)/shard_map/ppermute | solution.py:605
  80.4 12.3 %copy-start.73 = (f32[128]{0:T(128)S(1)}, f32[128]{0:T(128)}, u32[]{:S(2)}) copy-start(f32[128]{0:T(128)} %constant.118.clone) | copy-start | bytes 1540
  80.4 54.8 %all-to-all-start.1 = ((f32[32,8,2048]{2,1,0:T(8,128)}), f32[32,8,2048]{2,1,0:T(8,128)}, u32[]{:S(2)}, u32[]{:S(2)}) async-start(f32[32,8,2048]{2,1,0:T(8,128)} %bitcast.10), calls=%async_computation.1 | async-start | bytes 4194304 | tf_op jit(solution)/shard_map/all_to_all | solution.py:609
  89.5 15.6 %collective-permute-start.6 = (f32[4,4096]{1,0:T(4,128)S(1)}, f32[4,4096]{1,0:T(4,128)S(1)}, u32[]{:S(2)}, u32[]{:S(2)}) collective-permute-start(f32[4,4096]{1,0:T(4,128)S(1)} %bitcast.125), channel_id=1, source_target_pairs={{16,0}} | collective-permute-start | bytes 196616 | tf_op jit(solution)/shard_map/ppermute | solution.py:554
  108.4 31.4 %copy-start.14 = (f32[4,4,64,128]{3,2,1,0:T(8,128)}, f32[4,4,64,128]{3,2,1,0:T(8,128)S(1)}, u32[]{:S(2)}) copy-start(f32[4,4,64,128]{3,2,1,0:T(8,128)S(1)} %pad.21.clone) | copy-start | bytes 1572868
  110.2 29.6 %copy-start.16 = (f32[4,4,64,128]{3,2,1,0:T(8,128)}, f32[4,4,64,128]{3,2,1,0:T(8,128)S(1)}, u32[]{:S(2)}) copy-start(f32[4,4,64,128]{3,2,1,0:T(8,128)S(1)} %pad.22.clone) | copy-start | bytes 1572868
  135.2 29.5 %all-to-all-start.2 = ((f32[32,8,1024]{2,1,0:T(8,128)}), f32[32,8,1024]{2,1,0:T(8,128)S(1)}, u32[]{:S(2)}, u32[]{:S(2)}) async-start(f32[32,8,1024]{2,1,0:T(8,128)} %bitcast.23), calls=%async_computation.2 | async-start | bytes 2097152 | tf_op jit(solution)/shard_map/all_to_all | solution.py:609
  165.7 52.8 %all-to-all-start.3 = ((f32[32,8,2048]{2,1,0:T(8,128)}), f32[32,8,2048]{2,1,0:T(8,128)}, u32[]{:S(2)}, u32[]{:S(2)}) async-start(f32[32,8,2048]{2,1,0:T(8,128)} %bitcast.116), calls=%async_computation.3 | async-start | bytes 4194304 | tf_op jit(solution)/shard_map/all_to_all | solution.py:609
  234.3 29.5 %all-to-all-start.4 = ((f32[32,8,1024]{2,1,0:T(8,128)}), f32[32,8,1024]{2,1,0:T(8,128)S(1)}, u32[]{:S(2)}, u32[]{:S(2)}) async-start(f32[32,8,1024]{2,1,0:T(8,128)} %bitcast.28), calls=%async_computation.4 | async-start | bytes 2097152 | tf_op jit(solution)/shard_map/all_to_all | solution.py:609
  264.8 51.6 %all-to-all-start.5 = ((f32[32,8,2048]{2,1,0:T(8,128)}), f32[32,8,2048]{2,1,0:T(8,128)}, u32[]{:S(2)}, u32[]{:S(2)}) async-start(f32[32,8,2048]{2,1,0:T(8,128)} %bitcast.29), calls=%async_computation.5 | async-start | bytes 4194304 | tf_op jit(solution)/shard_map/all_to_all | solution.py:609
  316.4 29.5 %all-to-all-start.6 = ((f32[32,8,1024]{2,1,0:T(8,128)}), f32[32,8,1024]{2,1,0:T(8,128)S(1)}, u32[]{:S(2)}, u32[]{:S(2)}) async-start(f32[32,8,1024]{2,1,0:T(8,128)} %bitcast.31), calls=%async_computation.6 | async-start | bytes 2097152 | tf_op jit(solution)/shard_map/all_to_all | solution.py:609
  346.9 52.8 %all-to-all-start.7 = ((f32[32,8,2048]{2,1,0:T(8,128)}), f32[32,8,2048]{2,1,0:T(8,128)}, u32[]{:S(2)}, u32[]{:S(2)}) async-start(f32[32,8,2048]{2,1,0:T(8,128)} %bitcast.117), calls=%async_computation.7 | async-start | bytes 4194304 | tf_op jit(solution)/shard_map/all_to_all | solution.py:609
  409.0 19.7 %collective-permute-start.7 = (f32[3,64,512]{2,1,0:T(8,128)S(1)}, f32[3,64,512]{2,1,0:T(8,128)S(1)}, u32[]{:S(2)}, u32[]{:S(2)}) collective-permute-start(f32[3,64,512]{2,1,0:T(8,128)S(1)} %get-tuple-element.56), channel_id=1, source_target_pairs={{0,1},{1,0},{2,3},{3,2},{4,5},{5,4},{6,7},{7,6},{8,9},{9,8},{10,11... | collective-permute-start | bytes 1179656 | tf_op jit(solution)/shard_map/ppermute | solution.py:605
  412.7 29.7 %collective-permute-start.8 = (f32[3,64,512]{2,1,0:T(8,128)S(1)}, f32[3,64,512]{2,1,0:T(8,128)S(1)}, u32[]{:S(2)}, u32[]{:S(2)}) collective-permute-start(f32[3,64,512]{2,1,0:T(8,128)S(1)} %get-tuple-element.55), channel_id=1, source_target_pairs={{0,2},{1,3},{2,0},{3,1},{4,6},{5,7},{6,4},{7,5},{8,10},{9,11},{10,... | collective-permute-start | bytes 1179656 | tf_op jit(solution)/shard_map/ppermute | solution.py:605
  412.9 29.5 %collective-permute-start.9 = (f32[3,64,512]{2,1,0:T(8,128)S(1)}, f32[3,64,512]{2,1,0:T(8,128)S(1)}, u32[]{:S(2)}, u32[]{:S(2)}) collective-permute-start(f32[3,64,512]{2,1,0:T(8,128)S(1)} %get-tuple-element.54), channel_id=1, source_target_pairs={{0,3},{1,2},{2,1},{3,0},{4,7},{5,6},{6,5},{7,4},{8,11},{9,10},{10,... | collective-permute-start | bytes 1179656 | tf_op jit(solution)/shard_map/ppermute | solution.py:605
  415.3 27.2 %copy-start.58 = (f32[3,256,512]{2,1,0:T(8,128)S(1)}, f32[3,256,512]{2,1,0:T(8,128)}, u32[]{:S(2)}) copy-start(f32[3,256,512]{2,1,0:T(8,128)} %param.25) | copy-start | bytes 4718596
  415.3 27.2 %copy-start.63 = (f32[256,512]{1,0:T(8,128)S(1)}, f32[256,512]{1,0:T(8,128)}, u32[]{:S(2)}) copy-start(f32[256,512]{1,0:T(8,128)} %copy-done.62) | copy-start | bytes 1572868
  (69 other events, 288.8 us)
